TPU v7x, 128 devices: a whole 4x4x4 slice. The times are simulated.
128 devices in a mesh: gx: 8 (over x, core), gy: 16 (over y, z).
Axes of the slice: x: 4, y: 4, z: 4, core: 2. Of those that a mesh axis runs over, the one named last changes fastest.
Arguments:
- fine_start: float32 [3, 2048, 8192], P(None, 'gx', 'gy'), may hold values from -6 to 6
- fine_known: float32 [3, 2048, 8192], P(None, 'gx', 'gy'), may hold values from -18 to 18
- fine_mu: float32 [2048, 8192], P('gx', 'gy'), may hold values from 1 to 10
- coarse_start: float32 [3, 1024, 4096], P(None, ('gx', 'gy')), may hold values from -6 to 6
- coarse_known: float32 [3, 1024, 4096], P(None, ('gx', 'gy')), may hold values from -18 to 18
- coarse_mu: float32 [1024, 4096], P(('gx', 'gy')), may hold values from 1 to 10
Outputs:
- fine_ghost: float32 [3, 2048, 8192], P(None, 'gx', 'gy')
- coarse_ghost: float32 [3, 1024, 4096], P(None, ('gx', 'gy'))
- norms: float32 [3], replicated
All inputs are finite; a program needn't handle non-finite values.
Results may differ from a plain program's by a relative error of at most 0.0001.
Values sent between devices are 32-bit elements; how exact they have to be, the bound alone decides.
No kernel may reach another device: no remote copies, remote signals or barrier semaphores. Data moves between devices by JAX's collectives and lax.ppermute only.
A program may use at most 128 MiB of HBM per device.

v0:
```python
import jax
import jax.numpy as jnp
from jax import lax
from jax.experimental import pallas as pl
from jax.experimental.pallas import tpu as pltpu
from jax.sharding import PartitionSpec as P

ITERS = 3
GX, GY = "gx", "gy"
BOTH = (GX, GY)
PR = 128
TOP = 16
ROWS = PR + 2 * TOP
F32 = jnp.float32
BF16 = jnp.bfloat16
VMEM = pl.BlockSpec(memory_space=pltpu.VMEM)
SMEM = pl.BlockSpec(memory_space=pltpu.SMEM)
ANY = pl.BlockSpec(memory_space=pl.ANY)
LIMIT = 56 * 1024 * 1024


def shaped(*shape):
    return jax.ShapeDtypeStruct(shape, F32)


def params(**kw):
    return pltpu.CompilerParams(vmem_limit_bytes=LIMIT, **kw)


def cost(us, moved):
    return pl.CostEstimate(flops=int(us * 7.0e6), bytes_accessed=int(moved), transcendentals=0)


def lanes_of(rows):
    return lax.broadcasted_iota(jnp.int32, (rows, 128), 1)


def turn(x, shift):
    shift %= 128
    return x if shift == 0 else pltpu.roll(x, shift, axis=1)


MAIN = 120
TAIL = 40
HALO_ROWS = 17


def planes_of(start_ref, known_ref, mu_ref):
    def tile(p, t):
        cols = pl.ds(128 * t, 128)
        if p < 3:
            return start_ref[p, :, cols]
        if p < 6:
            return known_ref[p - 3, :, cols]
        return mu_ref[:, cols]

    return tile


def pack_kernel(first_ref, start_ref, known_ref, mu_ref, chunk_ref, edge_ref):
    tile = planes_of(start_ref, known_ref, mu_ref)
    lane = lanes_of(8)
    zero = jnp.zeros((8, 128), F32)
    first = first_ref[0] == 1

    def ends(x):
        return jnp.where(first, x[0:3], x[5:8])

    for j in range(16):
        side = zero
        for p in range(7):
            left = tile(p, 2 * j - 1) if j else zero
            right = tile(p, 2 * j + 2) if j < 15 else zero
            both = jnp.where(lane >= 125, left, right)
            side = jnp.where((lane >= 6 * p) & (lane < 6 * p + 6), turn(both, 6 * p + 3), side)
            for m in range(2):
                x = tile(p, 2 * j + m)
                chunk_ref[j, pl.ds((2 * p + m) * 8, 8), :] = x
                if p < 3:
                    edge_ref[j, pl.ds(m * HALO_ROWS + 3 * p, 3), :] = ends(x)
                else:
                    two = jnp.where(first, x[0:2], x[6:8])
                    edge_ref[j, pl.ds(m * HALO_ROWS + 3 + 2 * p, 2), :] = two
        chunk_ref[j, pl.ds(112, 8), :] = side
        edge_ref[j, pl.ds(2 * HALO_ROWS, 3), :] = ends(side)
        edge_ref[j, pl.ds(2 * HALO_ROWS + 3, 3), :] = jnp.zeros((3, 128), F32)


def tail_kernel(edge_ref, chunk_in, chunk_ref, sem):
    del chunk_in
    copy = pltpu.make_async_copy(edge_ref, chunk_ref.at[:, pl.ds(MAIN, TAIL), :], sem)
    copy.start()
    copy.wait()


def split3(x):
    a = x.astype(BF16)
    r = x - a.astype(F32)
    b = r.astype(BF16)
    return a, b, (r - b.astype(F32)).astype(BF16)


def permuted(x, table):
    a, b, c = split3(x)
    dot = lambda v: jnp.dot(v, table, preferred_element_type=F32)
    return dot(a) + dot(b) + dot(c)


def parity_table(forward):
    one = lax.broadcasted_iota(jnp.int32, (256, 256), 0 if forward else 1)
    two = lax.broadcasted_iota(jnp.int32, (256, 256), 1 if forward else 0)
    place = jnp.where(two < 128, 2 * two, 2 * two - 255)
    return jnp.where(one == place, 1.0, 0.0).astype(BF16)


def fine_kernel(
    start_hbm, known_hbm, mu_hbm, fs_ref, fk_ref, fm_ref, low_ref, high_ref, top_ref, bottom_ref, block, sems
):
    copies = []
    for k in range(7):
        source = (start_hbm.at[k] if k < 3 else None, known_hbm.at[k - 3] if 3 <= k < 6 else None, mu_hbm)[
            0 if k < 3 else 1 if k < 6 else 2
        ]
        for c in range(4):
            n = 4 * k + c
            copies.append(pltpu.make_async_copy(source.at[:, pl.ds(128 * c, 128)], block.at[k, c], sems.at[n]))
    for copy in copies:
        copy.start()
    table = parity_table(True)
    lane = lanes_of(PR)
    low_ref[...] = jnp.zeros((PR, 128), F32)
    high_ref[...] = jnp.zeros((PR, 128), F32)

    def put(ref, mask, value):
        ref[...] = jnp.where(mask, value, ref[...])

    for k in range(7):
        for copy in copies[4 * k : 4 * k + 4]:
            copy.wait()
        out, t0 = (fs_ref, fk_ref, fm_ref)[k // 3], 4 * k - 12 * (k // 3)
        for p in range(2):
            rows = pl.ds(p, PR, stride=2)
            for m in range(2):
                x = jnp.concatenate([block[k, 2 * m + c, rows, :] for c in range(2)], axis=1)
                y = permuted(x, table)
                for q in range(2):
                    t = t0 + 2 * p + q
                    v = y[:, 128 * q : 128 * q + 128]
                    out[t, m, :, :] = v
                    if k < 3:
                        top_ref[m, pl.ds(2 * t, 2), :] = v[0:2]
                        bottom_ref[m, pl.ds(2 * t, 2), :] = v[126:128]
                        if m == 0:
                            put(low_ref, (lane == 4 * t + 2) | (lane == 4 * t + 3), turn(v, 4 * t + 2))
                        else:
                            put(high_ref, (lane == 4 * t) | (lane == 4 * t + 1), turn(v, 4 * t - 126))
                    else:
                        row, at = (24 + t, 48 + 2 * t) if k < 6 else (36 + t, 72 + 2 * t)
                        top_ref[m, pl.ds(row, 1), :] = v[0:1]
                        bottom_ref[m, pl.ds(row, 1), :] = v[127:128]
                        if m == 0:
                            put(low_ref, lane == at + 1, turn(v, at + 1))
                        else:
                            put(high_ref, lane == at, turn(v, at - 127))


def start_side(x, t):
    lane = lanes_of(x.shape[0])
    return jnp.where((lane < 2) | (lane >= 126), turn(x, 126 - 4 * t), 0.0)


def other_side(x, at):
    lane = lanes_of(x.shape[0])
    return jnp.where((lane < 1) | (lane >= 127), turn(x, 127 - at), 0.0)


def rows_kernel(left_ref, right_ref, top_ref, bottom_ref, up_ref, down_ref):
    for part, out, two, one in ((top_ref, up_ref, 0, 0), (bottom_ref, down_ref, 126, 127)):
        out[0:2] = part[...]
        pair = left_ref[two : two + 2] + right_ref[two : two + 2]
        single = left_ref[one : one + 1] + right_ref[one : one + 1]
        for t in range(12):
            out[2, pl.ds(2 * t, 2), :] = start_side(pair, t)
            out[2, pl.ds(24 + t, 1), :] = other_side(single, 48 + 2 * t)
        for t in range(4):
            out[2, pl.ds(36 + t, 1), :] = other_side(single, 72 + 2 * t)


def sweep_kernel(
    fs_hbm, fk_hbm, fm_hbm, recv_ref, left_ref, right_ref, above_ref, below_ref,
    chunk_ref, fine_ref,
    ca, cb, kc, mc, rc, fa, fb, kf, mf, rf, sems,
):
    own = pl.ds(TOP, PR)
    copies = [
        pltpu.make_async_copy(src, dst.at[:, pl.ds(0, 2), own, :], sems.at[n])
        for n, (src, dst) in enumerate(((fs_hbm, fa), (fk_hbm, kf), (fm_hbm, mf)))
    ]
    for copy in copies:
        copy.start()
    zero8 = jnp.zeros((8, 128), F32)
    for ref, count in ((ca, 3), (cb, 3), (kc, 3), (fa, 12), (fb, 12), (kf, 12), (mf, 4)):
        for t in range(count):
            for m in range(3):
                for r in (0, 8, TOP + PR, TOP + PR + 8):
                    ref[t, m, pl.ds(r, 8), :] = zero8
    for m in range(3):
        for r in (0, 8, TOP + PR, TOP + PR + 8):
            mc[m, pl.ds(r, 8), :] = zero8
    lane8 = lanes_of(8)
    wide = (lane8 < 3) | (lane8 >= 125)

    def coarse(p):
        return (ca.at[p], kc.at[p - 3] if 3 <= p < 6 else None, mc)[0 if p < 3 else 1 if p < 6 else 2]

    for p in range(7):
        ref = coarse(p)
        for j in range(16):
            rows = pl.ds(TOP + 8 * j, 8)
            for m in range(2):
                ref[m, rows, :] = recv_ref[j, pl.ds((2 * p + m) * 8, 8), :]
            ref[2, rows, :] = jnp.where(wide, turn(recv_ref[j, pl.ds(112, 8), :], 125 - 6 * p), 0.0)
        count = 3 if p < 3 else 2
        h = 3 * p if p < 3 else 3 + 2 * p
        side = MAIN + 2 * HALO_ROWS
        for j, at, skip in ((0, TOP - count, 3 - count), (15, TOP + PR, 0)):
            rows = pl.ds(at, count)
            for m in range(2):
                ref[m, rows, :] = recv_ref[j, pl.ds(MAIN + m * HALO_ROWS + h, count), :]
            lane = lanes_of(count)
            halo = turn(recv_ref[j, pl.ds(side + skip, count), :], 125 - 6 * p)
            ref[2, rows, :] = jnp.where((lane < 3) | (lane >= 125), halo, 0.0)
    both = left_ref[...] + right_ref[...]
    for t in range(12):
        fa[t, 2, own, :] = start_side(both, t)
        kf[t, 2, own, :] = other_side(both, 48 + 2 * t)
    for t in range(4):
        mf[t, 2, own, :] = other_side(both, 72 + 2 * t)
    for m in range(3):
        for t in range(12):
            fa[t, m, pl.ds(TOP - 2, 2), :] = above_ref[m, pl.ds(2 * t, 2), :]
            fa[t, m, pl.ds(TOP + PR, 2), :] = below_ref[m, pl.ds(2 * t, 2), :]
            kf[t, m, pl.ds(TOP - 1, 1), :] = above_ref[m, pl.ds(24 + t, 1), :]
            kf[t, m, pl.ds(TOP + PR, 1), :] = below_ref[m, pl.ds(24 + t, 1), :]
        for t in range(4):
            mf[t, m, pl.ds(TOP - 1, 1), :] = above_ref[m, pl.ds(36 + t, 1), :]
            mf[t, m, pl.ds(TOP + PR, 1), :] = below_ref[m, pl.ds(36 + t, 1), :]
    for copy in copies:
        copy.wait()

    def inverse(i, _):
        r = pl.ds(pl.multiple_of(8 + 8 * i, 8), 8)
        for m in range(3):
            mu = mc[m, r, :]
            rc[m, r, :] = jnp.where(mu > 0.0, 1.0 / (mu + 1.0), 0.0)
            for t in range(4):
                mu = mf[t, m, r, :]
                rf[t, m, r, :] = jnp.where(mu > 0.0, 1.0 / (mu + 1.0), 0.0)
        return 0

    lax.fori_loop(0, ROWS // 8 - 2, inverse, 0)
    at_start, at_end = lane8 == 0, lane8 == 127

    def before(x, tiles):
        turned = [turn(v, 1) for v in x]
        return [jnp.where(at_start, turned[m - 1], turned[m]) for m in tiles]

    def after(x, tiles):
        turned = [turn(v, 127) for v in x]
        return [jnp.where(at_end, turned[(m + 1) % 3], turned[m]) for m in tiles]

    def step(r, c_old, f_old, store_c, store_f, tiles, sums):
        here, up, down = pl.ds(r, 8), pl.ds(r - 1, 8), pl.ds(r + 1, 8)
        every = range(3)
        totals = [zero8] * 4
        for k in range(3):
            c = [c_old[k, m, here, :] for m in every]
            cu = [c_old[k, m, up, :] for m in every]
            cd = [c_old[k, m, down, :] for m in every]
            cw, ce = before(c, tiles), after(c, tiles)
            f = [[[f_old[4 * k + 2 * p + q, m, here, :] for m in every] for q in range(2)] for p in range(2)]
            for p in range(2):
                row = [0.375 * c[m] + 0.125 * (cu, cd)[p][m] for m in every]
                quarter = [0.25 * v for v in row]
                for q in range(2):
                    t = 4 * k + 2 * p + q
                    beside = (before, after)[q](quarter, tiles)
                    far = (before, after)[q](f[p][1 - q], tiles)
                    for n, m in enumerate(tiles):
                        v = f[p][q][m]
                        other = f_old[4 * k + 2 * (1 - p) + q, m, (up, down)[p], :]
                        near = (f[1 - p][q][m] + other) + (f[p][1 - q][m] + far[n])
                        s = (kf[t, m, here, :] + 0.25 * near) + (0.75 * row[m] + beside[n])
                        store_f(t, m, s * rf[2 * p + q, m, here, :])
                        if sums and m < 2:
                            res = s - (mf[2 * p + q, m, here, :] + 1.0) * v
                            totals[2 * p + q] = totals[2 * p + q] + res * res
            for n, m in enumerate(tiles):
                near = (cu[m] + cd[m]) + (cw[n] + ce[n])
                four = (f[0][0][m] + f[0][1][m]) + (f[1][0][m] + f[1][1][m])
                s = (kc[k, m, here, :] + 0.25 * near) + 0.125 * four
                store_c(k, m, s * rc[m, here, :])
                if sums and m < 2:
                    res = s - (mc[m, here, :] + 1.0) * c[m]
                    totals[k] = totals[k] + res * res
        return (totals[0] + totals[1]) + (totals[2] + totals[3])

    def sweep(c_old, f_old, c_new, f_new):
        def store(r):
            def store_c(k, m, v):
                c_new[k, m, pl.ds(r, 8), :] = v

            def store_f(t, m, v):
                f_new[t, m, pl.ds(r, 8), :] = v

            return store_c, store_f

        def body(i, total):
            r = pl.multiple_of(TOP + 8 * i, 8)
            return total + step(r, c_old, f_old, *store(r), range(3), True)

        total = lax.fori_loop(0, PR // 8, body, zero8)

        def edge(i, carry):
            r = pl.multiple_of(TOP - 8 + i * (PR + 8), 8)
            step(r, c_old, f_old, *store(r), range(3), False)
            return carry

        lax.fori_loop(0, 2, edge, 0)
        return total

    totals = [sweep(ca, fa, cb, fb), sweep(cb, fb, ca, fa)]

    def last(i, total):
        r = pl.multiple_of(TOP + 8 * i, 8)

        def store_c(k, m, v):
            chunk_ref[i, pl.ds((2 * k + m) * 8, 8), :] = v

        def store_f(t, m, v):
            fine_ref[t, m, pl.ds(pl.multiple_of(8 * i, 8), 8), :] = v

        return total + step(r, ca, fa, store_c, store_f, range(2), True)

    totals.append(lax.fori_loop(0, PR // 8, last, zero8))
    sums = jnp.concatenate([jnp.sum(v, axis=0, keepdims=True) for v in totals] + [jnp.zeros((5, 128), F32)], axis=0)
    for j in range(16):
        chunk_ref[j, pl.ds(48, 8), :] = sums


def join_kernel(fine_ref, out_hbm, block, sems):
    table = parity_table(False)
    copies = []
    for k in range(3):
        for m in range(2):
            for p in range(2):
                x = jnp.concatenate([fine_ref[4 * k + 2 * p + q, m, :, :] for q in range(2)], axis=1)
                y = permuted(x, table)
                for c in range(2):
                    block[k, 2 * m + c, pl.ds(p, PR, stride=2), :] = y[:, 128 * c : 128 * c + 128]
            for c in range(2 * m, 2 * m + 2):
                copy = pltpu.make_async_copy(
                    block.at[k, c], out_hbm.at[k, :, pl.ds(128 * c, 128)], sems.at[4 * k + c]
                )
                copy.start()
                copies.append(copy)
    for copy in copies:
        copy.wait()


def sum_kernel(recv_ref, out_ref):
    total = recv_ref[0]
    for j in range(1, 16):
        total = total + recv_ref[j]
    for i in range(8):
        out_ref[i] = total


def coarse_kernel(recv_ref, out_ref):
    for j in range(16):
        for k in range(3):
            for m in range(2):
                out_ref[k, :, pl.ds(256 * j + 128 * m, 128)] = recv_ref[j, pl.ds((2 * k + m) * 8, 8), :]


def on_device(fine_start, fine_known, fine_mu, coarse_start, coarse_known, coarse_mu):
    count_x, count_y = lax.axis_size(GX), lax.axis_size(GY)
    cell_total = 3.0 * (fine_mu.size + coarse_mu.size) * (count_x * count_y)
    first = (lax.axis_index(GY) == 0).astype(jnp.int32).reshape(1)

    chunk, edge = pl.pallas_call(
        pack_kernel,
        out_shape=(shaped(16, MAIN + TAIL, 128), shaped(16, TAIL, 128)),
        in_specs=[SMEM, VMEM, VMEM, VMEM],
        out_specs=(VMEM, VMEM),
        compiler_params=params(),
        cost_estimate=cost(2, 2.5e6),
        name="pack",
    )(first, coarse_start, coarse_known, coarse_mu)
    pairs = [(i * count_y + count_y - 1, (i + 1) * count_y) for i in range(count_x - 1)]
    edge = lax.ppermute(edge, BOTH, pairs + [(b, a) for a, b in pairs])
    chunk = pl.pallas_call(
        tail_kernel,
        out_shape=shaped(16, MAIN + TAIL, 128),
        in_specs=[VMEM, ANY],
        out_specs=ANY,
        scratch_shapes=[pltpu.SemaphoreType.DMA(())],
        input_output_aliases={1: 0},
        compiler_params=params(),
        cost_estimate=cost(1, 0.6e6),
        name="tail",
    )(edge, chunk)
    recv = lax.all_to_all(chunk, GY, 0, 0, tiled=True)

    fs, fk, fm, low, high, top, bottom = pl.pallas_call(
        fine_kernel,
        out_shape=(
            shaped(12, 2, PR, 128), shaped(12, 2, PR, 128), shaped(4, 2, PR, 128),
            shaped(PR, 128), shaped(PR, 128), shaped(2, 40, 128), shaped(2, 40, 128),
        ),
        in_specs=[ANY] * 3,
        out_specs=(VMEM,) * 7,
        scratch_shapes=[pltpu.VMEM((7, 4, 2 * PR, 128), F32), pltpu.SemaphoreType.DMA((28,))],
        compiler_params=params(),
        cost_estimate=cost(4, 7e6),
        name="fine",
    )(fine_start, fine_known, fine_mu)

    def ahead(n):
        return [(i, i + 1) for i in range(n - 1)]

    def back(n):
        return [(i + 1, i) for i in range(n - 1)]

    left = lax.ppermute(high, GY, ahead(count_y))
    right = lax.ppermute(low, GY, back(count_y))
    up, down = pl.pallas_call(
        rows_kernel,
        out_shape=(shaped(3, 40, 128),) * 2,
        in_specs=[VMEM] * 4,
        out_specs=(VMEM,) * 2,
        compiler_params=params(),
        cost_estimate=cost(1, 0.3e6),
        name="rows",
    )(left, right, top, bottom)
    above = lax.ppermute(down, GX, ahead(count_x))
    below = lax.ppermute(up, GX, back(count_x))

    chunk, fine = pl.pallas_call(
        sweep_kernel,
        out_shape=(shaped(16, 56, 128), shaped(12, 2, PR, 128)),
        in_specs=[ANY] * 3 + [VMEM] * 5,
        out_specs=(VMEM,) * 2,
        scratch_shapes=[
            pltpu.VMEM((3, 3, ROWS, 128), F32),
            pltpu.VMEM((3, 3, ROWS, 128), F32),
            pltpu.VMEM((3, 3, ROWS, 128), F32),
            pltpu.VMEM((3, ROWS, 128), F32),
            pltpu.VMEM((3, ROWS, 128), F32),
            pltpu.VMEM((12, 3, ROWS, 128), F32),
            pltpu.VMEM((12, 3, ROWS, 128), F32),
            pltpu.VMEM((12, 3, ROWS, 128), F32),
            pltpu.VMEM((4, 3, ROWS, 128), F32),
            pltpu.VMEM((4, 3, ROWS, 128), F32),
            pltpu.SemaphoreType.DMA((3,)),
        ],
        compiler_params=params(),
        cost_estimate=cost(8, 7e6),
        name="sweeps",
    )(fs, fk, fm, recv, left, right, above, below)
    out = lax.all_to_all(chunk, GY, 0, 0, tiled=True)

    fine_ghost = pl.pallas_call(
        join_kernel,
        out_shape=shaped(*fine_start.shape),
        in_specs=[VMEM],
        out_specs=ANY,
        scratch_shapes=[pltpu.VMEM((3, 4, 2 * PR, 128), F32), pltpu.SemaphoreType.DMA((12,))],
        compiler_params=params(),
        cost_estimate=cost(2, 3e6),
        name="join",
    )(fine)
    sums = pl.pallas_call(
        sum_kernel,
        grid=(1,),
        out_shape=shaped(8, 8, 128),
        in_specs=[pl.BlockSpec((16, 8, 128), lambda i: (0, 6, 0))],
        out_specs=pl.BlockSpec((8, 8, 128), lambda i: (0, 0, 0)),
        compiler_params=params(),
        cost_estimate=cost(1, 0.1e6),
        name="sums",
    )(out)
    sums = lax.all_to_all(sums, GX, 0, 0, tiled=True)
    coarse_ghost = pl.pallas_call(
        coarse_kernel,
        out_shape=shaped(*coarse_start.shape),
        in_specs=[VMEM],
        out_specs=VMEM,
        compiler_params=params(),
        cost_estimate=cost(1, 0.8e6),
        name="coarse",
    )(out)
    norms = jnp.sqrt(jnp.sum(sums[:, :ITERS, :], axis=(0, 2)) / cell_total)
    return fine_ghost, coarse_ghost, norms


def solution(mesh):
    fine, coarse = P(None, GX, GY), P(None, BOTH, None)
    return jax.shard_map(
        on_device,
        mesh=mesh,
        in_specs=(fine, fine, P(GX, GY), coarse, coarse, P(BOTH, None)),
        out_specs=(fine, coarse, P()),
        check_vma=False,
    )
```

profile of v0, /device:TPU:1, one launch (start us, length us, event | category | flops | bytes accessed | tf_op | source)
XLA Modules:
  0.0 102.9 jit_solution(3761361047935617467)
XLA Ops:
  0.6 2.5 %pack.1 = (f32[16,160,128]{2,1,0:T(8,128)}, f32[16,40,128]{2,1,0:T(8,128)}) custom-call(s32[1]{0:T(128)} %bitcast.first_ref, f32[3,8,4096]{2,1,0:T(8,128)} %start_ref.1, f32[3,8,4096]{2,1,0:T(8,128)} %known_ref.1, f32[8,4096]{1,0:T(8,128)} %mu_ref.1), custom_call_target="tpu_custom_call" | custom-call | flops 14000000 | bytes 2500000 | tf_op jit(solution)/shard_map/pack/pallas_call | solution.py:391
  3.2 9.5 %collective-permute-start = (f32[16,40,128]{2,1,0:T(8,128)}, f32[16,40,128]{2,1,0:T(8,128)S(1)}, u32[]{:S(2)}, u32[]{:S(2)}) collective-permute-start(f32[16,40,128]{2,1,0:T(8,128)} %get-tuple-element.19), channel_id=1, source_target_pairs={{15,16},{31,32},{47,48},{63,64},{79,80},{95,96},{111,112},{16,15},... | collective-permute-start | bytes 983048 | tf_op jit(solution)/shard_map/ppermute | solution.py:401
  12.7 7.8 %collective-permute-done.edge_ref = f32[16,40,128]{2,1,0:T(8,128)S(1)} collective-permute-done((f32[16,40,128]{2,1,0:T(8,128)}, f32[16,40,128]{2,1,0:T(8,128)S(1)}, u32[]{:S(2)}, u32[]{:S(2)}) %collective-permute-start) | collective-permute-done | bytes 327712 | tf_op jit(solution)/shard_map/ppermute | solution.py:401
  20.5 0.7 copy-done.1
  21.2 1.8 %tail.1 = f32[16,160,128]{2,1,0:T(8,128)} custom-call(f32[16,40,128]{2,1,0:T(8,128)} %copy-done.1, f32[16,160,128]{2,1,0:T(8,128)} %get-tuple-element.20.chunk_in), custom_call_target="tpu_custom_call", output_to_operand_aliasing={{}: (1, {})} | custom-call | flops 7000000 | bytes 600000 | tf_op jit(solution)/shard_map/tail/pallas_call | solution.py:402
  23.0 4.0 %all-to-all-start = ((f32[16,160,128]{2,1,0:T(8,128)}), f32[16,160,128]{2,1,0:T(8,128)S(1)}, u32[]{:S(2)}, u32[]{:S(2)}) async-start(f32[16,160,128]{2,1,0:T(8,128)} %tail.1), calls=%async_computation | async-start | bytes 2621440 | tf_op jit(solution)/shard_map/all_to_all | solution.py:413
  27.0 6.2 %fine.1 = (f32[12,2,128,128]{3,2,1,0:T(8,128)}, f32[12,2,128,128]{3,2,1,0:T(8,128)}, f32[4,2,128,128]{3,2,1,0:T(8,128)}, f32[128,128]{1,0:T(8,128)}, f32[128,128...) custom-call(f32[3,256,512]{2,1,0:T(8,128)} %start_hbm.1, f32[3,256,512]{2,1,0:T(8,128)} %known_hbm.1, ...), custom_call_target="tpu_custom_call" | custom-call | flops 28000000 | bytes 7000000 | tf_op jit(solution)/shard_map/fine/pallas_call | solution.py:415
  33.2 3.3 %collective-permute-start.1 = (f32[128,128]{1,0:T(8,128)}, f32[128,128]{1,0:T(8,128)S(1)}, u32[]{:S(2)}, u32[]{:S(2)}) collective-permute-start(f32[128,128]{1,0:T(8,128)} %get-tuple-element.21), channel_id=1, source_target_pairs={{0,1},{1,2},{2,3},{3,4},{4,5},{5,6},{6,7},{7,8},{8,9},{9,10},{10,1... | collective-permute-start | bytes 196616 | tf_op jit(solution)/shard_map/ppermute | solution.py:435
  36.5 1.3 %collective-permute-start.2 = (f32[128,128]{1,0:T(8,128)}, f32[128,128]{1,0:T(8,128)S(1)}, u32[]{:S(2)}, u32[]{:S(2)}) collective-permute-start(f32[128,128]{1,0:T(8,128)} %get-tuple-element.22), channel_id=1, source_target_pairs={{1,0},{2,1},{3,2},{4,3},{5,4},{6,5},{7,6},{8,7},{9,8},{10,9},{11,1... | collective-permute-start | bytes 196616 | tf_op jit(solution)/shard_map/ppermute | solution.py:436
  37.8 6.5 %collective-permute-done.1.left_ref = f32[128,128]{1,0:T(8,128)S(1)} collective-permute-done((f32[128,128]{1,0:T(8,128)}, f32[128,128]{1,0:T(8,128)S(1)}, u32[]{:S(2)}, u32[]{:S(2)}) %collective-permute-start.1) | collective-permute-done | bytes 65568 | tf_op jit(solution)/shard_map/ppermute | solution.py:435
  44.3 1.6 %collective-permute-done.2.right_ref = f32[128,128]{1,0:T(8,128)S(1)} collective-permute-done((f32[128,128]{1,0:T(8,128)}, f32[128,128]{1,0:T(8,128)S(1)}, u32[]{:S(2)}, u32[]{:S(2)}) %collective-permute-start.2) | collective-permute-done | bytes 65568 | tf_op jit(solution)/shard_map/ppermute | solution.py:436
  45.9 0.6 copy-done.3
  46.5 1.6 %rows.1 = (f32[3,40,128]{2,1,0:T(8,128)}, f32[3,40,128]{2,1,0:T(8,128)}) custom-call(f32[128,128]{1,0:T(8,128)} %copy-done.2, f32[128,128]{1,0:T(8,128)} %copy-done.3, f32[2,40,128]{2,1,0:T(8,128)} %get-tuple-element.23.top_ref, f32[2,40,128]{2,1,0:T(8,128)} %get-tuple-element.24.bottom_ref), custom_call_target="tpu_custom_call" | custom-call | flops 7000000 | bytes 300000 | tf_op jit(solution)/shard_map/rows/pallas_call | solution.py:437
  48.1 4.1 %collective-permute-start.3 = (f32[3,40,128]{2,1,0:T(8,128)}, f32[3,40,128]{2,1,0:T(8,128)S(1)}, u32[]{:S(2)}, u32[]{:S(2)}) collective-permute-start(f32[3,40,128]{2,1,0:T(8,128)} %get-tuple-element.25), channel_id=1, source_target_pairs={{0,16},{16,32},{32,48},{48,64},{64,80},{80,96},{96,112},{1,17},{17... | collective-permute-start | bytes 184328 | tf_op jit(solution)/shard_map/ppermute | solution.py:446
  52.2 1.9 %collective-permute-start.4 = (f32[3,40,128]{2,1,0:T(8,128)}, f32[3,40,128]{2,1,0:T(8,128)S(1)}, u32[]{:S(2)}, u32[]{:S(2)}) collective-permute-start(f32[3,40,128]{2,1,0:T(8,128)} %get-tuple-element.26), channel_id=1, source_target_pairs={{16,0},{32,16},{48,32},{64,48},{80,64},{96,80},{112,96},{17,1},{33... | collective-permute-start | bytes 184328 | tf_op jit(solution)/shard_map/ppermute | solution.py:447
  54.1 3.8 %collective-permute-done.4.below_ref = f32[3,40,128]{2,1,0:T(8,128)S(1)} collective-permute-done((f32[3,40,128]{2,1,0:T(8,128)}, f32[3,40,128]{2,1,0:T(8,128)S(1)}, u32[]{:S(2)}, u32[]{:S(2)}) %collective-permute-start.4) | collective-permute-done | bytes 61472 | tf_op jit(solution)/shard_map/ppermute | solution.py:447
  57.9 0.6 copy-done.5
  59.0 14.6 %sweeps.1 = (f32[16,56,128]{2,1,0:T(8,128)}, f32[12,2,128,128]{3,2,1,0:T(8,128)}) custom-call(f32[12,2,128,128]{3,2,1,0:T(8,128)} %get-tuple-element.16.fs_hbm, f32[12,2,128,128]{3,2,1,0:T(8,128)} %get-tuple-element.17.fk_hbm, f32[4,2,128,128]{3,2,1,0:T(8,128)} %get-tuple-element.18.fm_hbm, f32[16,160,128]{2,1,0:T(8,128)} %copy-done, f32[128,128]{1,0:T(8,128)} %copy-done.2, ...), custom_call_target="tpu_custom_call" | custom-call | flops 56000000 | bytes 7000000 | tf_op jit(solution)/shard_map/sweeps/pallas_call | solution.py:449
  73.6 17.5 %all_to_all.15.recv_ref = f32[16,56,128]{2,1,0:T(8,128)} all-to-all(f32[16,56,128]{2,1,0:T(8,128)} %get-tuple-element.28), channel_id=1, replica_groups=mesh['gx'=8,'gy'=16] {'gy'}, dimensions={0} | all-to-all | bytes 917504 | tf_op jit(solution)/shard_map/all_to_all | solution.py:471
  91.1 1.5 %sums.1 = f32[8,8,128]{2,1,0:T(8,128)} custom-call(f32[16,56,128]{2,1,0:T(8,128)} %all_to_all.15.recv_ref), custom_call_target="tpu_custom_call" | custom-call | flops 7000000 | bytes 100000 | tf_op jit(solution)/shard_map/sums/pallas_call | solution.py:483
  92.6 4.8 %all-to-all-start.2 = ((f32[8,8,128]{2,1,0:T(8,128)}), f32[8,8,128]{2,1,0:T(8,128)S(1)}, u32[]{:S(2)}, u32[]{:S(2)}) async-start(f32[8,8,128]{2,1,0:T(8,128)} %sums.1), calls=%async_computation.2 | async-start | bytes 65536 | tf_op jit(solution)/shard_map/all_to_all | solution.py:493
  97.4 3.0 %join.1 = f32[3,256,512]{2,1,0:T(8,128)} custom-call(f32[12,2,128,128]{3,2,1,0:T(8,128)} %get-tuple-element.27.fine_ref), custom_call_target="tpu_custom_call" | custom-call | flops 14000000 | bytes 3000000 | tf_op jit(solution)/shard_map/join/pallas_call | solution.py:473
  100.5 1.8 %coarse.1 = f32[3,8,4096]{2,1,0:T(8,128)} custom-call(f32[16,56,128]{2,1,0:T(8,128)} %all_to_all.15.recv_ref), custom_call_target="tpu_custom_call" | custom-call | flops 7000000 | bytes 800000 | tf_op jit(solution)/shard_map/coarse/pallas_call | solution.py:494
  102.4 0.5 multiply_sqrt_fusion
  (13 shorter events, 0.6 us)
Async XLA Ops:
  3.2 17.3 %collective-permute-start = (f32[16,40,128]{2,1,0:T(8,128)}, f32[16,40,128]{2,1,0:T(8,128)S(1)}, u32[]{:S(2)}, u32[]{:S(2)}) collective-permute-start(f32[16,40,128]{2,1,0:T(8,128)} %get-tuple-element.19), channel_id=1, source_target_pairs={{15,16},{31,32},{47,48},{63,64},{79,80},{95,96},{111,112},{16,15},... | collective-permute-start | bytes 983048 | tf_op jit(solution)/shard_map/ppermute | solution.py:401
  20.5 0.7 copy-start.1
  23.0 34.9 %all-to-all-start = ((f32[16,160,128]{2,1,0:T(8,128)}), f32[16,160,128]{2,1,0:T(8,128)S(1)}, u32[]{:S(2)}, u32[]{:S(2)}) async-start(f32[16,160,128]{2,1,0:T(8,128)} %tail.1), calls=%async_computation | async-start | bytes 2621440 | tf_op jit(solution)/shard_map/all_to_all | solution.py:413
  33.2 11.1 %collective-permute-start.1 = (f32[128,128]{1,0:T(8,128)}, f32[128,128]{1,0:T(8,128)S(1)}, u32[]{:S(2)}, u32[]{:S(2)}) collective-permute-start(f32[128,128]{1,0:T(8,128)} %get-tuple-element.21), channel_id=1, source_target_pairs={{0,1},{1,2},{2,3},{3,4},{4,5},{5,6},{6,7},{7,8},{8,9},{9,10},{10,1... | collective-permute-start | bytes 196616 | tf_op jit(solution)/shard_map/ppermute | solution.py:435
  36.5 9.4 %collective-permute-start.2 = (f32[128,128]{1,0:T(8,128)}, f32[128,128]{1,0:T(8,128)S(1)}, u32[]{:S(2)}, u32[]{:S(2)}) collective-permute-start(f32[128,128]{1,0:T(8,128)} %get-tuple-element.22), channel_id=1, source_target_pairs={{1,0},{2,1},{3,2},{4,3},{5,4},{6,5},{7,6},{8,7},{9,8},{10,9},{11,1... | collective-permute-start | bytes 196616 | tf_op jit(solution)/shard_map/ppermute | solution.py:436
  44.3 1.6 %copy-start.2 = (f32[128,128]{1,0:T(8,128)}, f32[128,128]{1,0:T(8,128)S(1)}, u32[]{:S(2)}) copy-start(f32[128,128]{1,0:T(8,128)S(1)} %collective-permute-done.1.left_ref) | copy-start | bytes 196612
  45.9 0.6 copy-start.3
  48.1 6.0 %collective-permute-start.3 = (f32[3,40,128]{2,1,0:T(8,128)}, f32[3,40,128]{2,1,0:T(8,128)S(1)}, u32[]{:S(2)}, u32[]{:S(2)}) collective-permute-start(f32[3,40,128]{2,1,0:T(8,128)} %get-tuple-element.25), channel_id=1, source_target_pairs={{0,16},{16,32},{32,48},{48,64},{64,80},{80,96},{96,112},{1,17},{17... | collective-permute-start | bytes 184328 | tf_op jit(solution)/shard_map/ppermute | solution.py:446
  52.2 5.8 %collective-permute-start.4 = (f32[3,40,128]{2,1,0:T(8,128)}, f32[3,40,128]{2,1,0:T(8,128)S(1)}, u32[]{:S(2)}, u32[]{:S(2)}) collective-permute-start(f32[3,40,128]{2,1,0:T(8,128)} %get-tuple-element.26), channel_id=1, source_target_pairs={{16,0},{32,16},{48,32},{64,48},{80,64},{96,80},{112,96},{17,1},{33... | collective-permute-start | bytes 184328 | tf_op jit(solution)/shard_map/ppermute | solution.py:447
  54.1 3.8 %copy-start.4 = (f32[3,40,128]{2,1,0:T(8,128)}, f32[3,40,128]{2,1,0:T(8,128)S(1)}, u32[]{:S(2)}) copy-start(f32[3,40,128]{2,1,0:T(8,128)S(1)} %collective-permute-done.3.above_ref) | copy-start | bytes 184324
  57.9 0.6 copy-start.5
  57.9 1.1 %copy-start = (f32[16,160,128]{2,1,0:T(8,128)}, f32[16,160,128]{2,1,0:T(8,128)S(1)}, u32[]{:S(2)}) copy-start(f32[16,160,128]{2,1,0:T(8,128)S(1)} %all-to-all-done.recv_ref) | copy-start | bytes 3932164
  92.6 9.7 %all-to-all-start.2 = ((f32[8,8,128]{2,1,0:T(8,128)}), f32[8,8,128]{2,1,0:T(8,128)S(1)}, u32[]{:S(2)}, u32[]{:S(2)}) async-start(f32[8,8,128]{2,1,0:T(8,128)} %sums.1), calls=%async_computation.2 | async-start | bytes 65536 | tf_op jit(solution)/shard_map/all_to_all | solution.py:493
where the time goes:
time: 104 us; the launch traced here: 103 us
  Pallas kernels  33 us (32%)
  starting transfers between devices  28.9 us (28%)
  waiting for transfers between devices  19.7 us (19%)
  blocking collectives  17.5 us (17%)
  local copies, waits for them, and re-layouts  2.43 us (2%)
    all_to_all x1, blocking collectives, on_device(): out = lax.all_to_all(chunk, GY, 0, 0, tiled=True)  17.5 us
    pallas_call x1, Pallas kernels, on_device(): pl.pallas_call(sweep_kernel, out_shape=(shaped(16, 56, 128), shaped(12, 2...  14.6 us
    ppermute x1, starting transfers between devices, on_device(): edge = lax.ppermute(edge, BOTH, pairs + [(b, a) for a, b in pairs])  9.48 us
    ppermute x1, waiting for transfers between devices, on_device(): edge = lax.ppermute(edge, BOTH, pairs + [(b, a) for a, b in pairs])  7.82 us
    ppermute x1, waiting for transfers between devices, on_device(): left = lax.ppermute(high, GY, ahead(count_y))  6.49 us
    pallas_call x1, Pallas kernels, on_device(): pl.pallas_call(fine_kernel, out_shape=(shaped(12, 2, PR, 128), shaped(12,...  6.17 us
    all_to_all x1, starting transfers between devices, on_device(): sums = lax.all_to_all(sums, GX, 0, 0, tiled=True)  4.84 us
    ppermute x1, starting transfers between devices, on_device(): above = lax.ppermute(down, GX, ahead(count_x))  4.05 us
  transfers between devices with their start and end apart: 7, of which 4 were waited for; matrix products, arithmetic and copies ran while one was open for 0% of the time, Pallas kernels for 12%

commit v1 on v0

v1 whole, which is shorter than its diff:
```python
import jax
import jax.numpy as jnp
from jax import lax
from jax.experimental import pallas as pl
from jax.experimental.pallas import tpu as pltpu
from jax.sharding import PartitionSpec as P

ITERS = 3
GX, GY = "gx", "gy"
BOTH = (GX, GY)
PR = 128
TOP = 16
ROWS = PR + 2 * TOP
F32 = jnp.float32
BF16 = jnp.bfloat16
VMEM = pl.BlockSpec(memory_space=pltpu.VMEM)
HBM = pl.BlockSpec(memory_space=pltpu.HBM)


def shaped(*shape):
    return jax.ShapeDtypeStruct(shape, F32)


ALL_KIB = 65472


def params(kib):
    return pltpu.CompilerParams(vmem_limit_bytes=kib << 10)


def cost(us, moved):
    return pl.CostEstimate(flops=int(us * 7.0e6), bytes_accessed=int(moved), transcendentals=0)


def in_hbm(*arrays):
    return tuple(pltpu.with_memory_space_constraint(a, pltpu.HBM) for a in arrays)


def lanes_of(rows):
    return lax.broadcasted_iota(jnp.int32, (rows, 128), 1)


def turn(x, shift):
    shift %= 128
    return x if shift == 0 else pltpu.roll(x, shift, axis=1)


MAIN = 120
EDGE = 64


def edge_rows(p):
    return (40 + 3 * p, 3) if p < 3 else (43 + 2 * p, 2)


def planes_of(start_ref, known_ref, mu_ref):
    def tile(p, t):
        cols = pl.ds(128 * t, 128)
        if p < 3:
            return start_ref[p, :, cols]
        if p < 6:
            return 4.0 * known_ref[p - 3, :, cols]
        return 4.0 * mu_ref[:, cols]

    return tile


def pack_kernel(start_hbm, known_hbm, mu_hbm, chunk_ref, start_ref, known_ref, mu_ref, sems):
    copies = [
        pltpu.make_async_copy(src, dst, sems.at[n])
        for n, (src, dst) in enumerate(((start_hbm, start_ref), (known_hbm, known_ref), (mu_hbm, mu_ref)))
    ]
    for copy in copies:
        copy.start()
    for copy in copies:
        copy.wait()
    tile = planes_of(start_ref, known_ref, mu_ref)
    lane = lanes_of(8)
    zero = jnp.zeros((8, 128), F32)
    for j in range(16):
        side = zero
        for p in range(7):
            left = tile(p, 2 * j - 1) if j else zero
            right = tile(p, 2 * j + 2) if j < 15 else zero
            both = jnp.where(lane >= 125, left, right)
            side = jnp.where((lane >= 6 * p) & (lane < 6 * p + 6), turn(both, 6 * p + 3), side)
            for m in range(2):
                chunk_ref[j, pl.ds((2 * p + m) * 8, 8), :] = tile(p, 2 * j + m)
        chunk_ref[j, pl.ds(112, 8), :] = side


def beside(x, p):
    lane = lanes_of(x.shape[0])
    return jnp.where((lane < 3) | (lane >= 125), turn(x, 125 - 6 * p), 0.0)


def split3(x):
    a = x.astype(BF16)
    r = x - a.astype(F32)
    b = r.astype(BF16)
    return a, b, (r - b.astype(F32)).astype(BF16)


def permuted(x, table):
    a, b, c = split3(x)
    dot = lambda v: jnp.dot(v, table, preferred_element_type=F32)
    return dot(a) + dot(b) + dot(c)


def parity_table(forward, value=1.0):
    one = lax.broadcasted_iota(jnp.int32, (256, 256), 0 if forward else 1)
    two = lax.broadcasted_iota(jnp.int32, (256, 256), 1 if forward else 0)
    place = jnp.where(two < 128, 2 * two, 2 * two - 255)
    return jnp.where(one == place, value, 0.0).astype(BF16)


def fine_kernel(
    start_hbm, known_hbm, mu_hbm, fs_hbm, fk_hbm, fm_hbm, low_ref, high_ref, top_ref, bottom_ref,
    block, planes, sems, out_sems,
):
    copies = []
    for k in range(7):
        source = (start_hbm.at[k] if k < 3 else None, known_hbm.at[k - 3] if 3 <= k < 6 else None, mu_hbm)[
            0 if k < 3 else 1 if k < 6 else 2
        ]
        for c in range(4):
            n = 4 * k + c
            copies.append(pltpu.make_async_copy(source.at[:, pl.ds(128 * c, 128)], block.at[k, c], sems.at[n]))
    for copy in copies:
        copy.start()
    tables = parity_table(True), parity_table(True, 4.0)
    lane = lanes_of(PR)
    low_ref[...] = jnp.zeros((PR, 128), F32)
    high_ref[...] = jnp.zeros((PR, 128), F32)

    def put(ref, mask, value):
        ref[...] = jnp.where(mask, value, ref[...])

    written = []
    for k in range(7):
        for copy in copies[4 * k : 4 * k + 4]:
            copy.wait()
        out, t0 = (fs_hbm, fk_hbm, fm_hbm)[k // 3], 4 * k - 12 * (k // 3)
        for p in range(2):
            rows = pl.ds(p, PR, stride=2)
            for m in range(2):
                x = jnp.concatenate([block[k, 2 * m + c, rows, :] for c in range(2)], axis=1)
                y = permuted(x, tables[k >= 3])
                for q in range(2):
                    t = t0 + 2 * p + q
                    v = y[:, 128 * q : 128 * q + 128]
                    planes[4 * k + 2 * p + q, m, :, :] = v
                    if k < 3:
                        top_ref[m, pl.ds(2 * t, 2), :] = v[0:2]
                        bottom_ref[m, pl.ds(2 * t, 2), :] = v[126:128]
                        if m == 0:
                            put(low_ref, (lane == 4 * t + 2) | (lane == 4 * t + 3), turn(v, 4 * t + 2))
                        else:
                            put(high_ref, (lane == 4 * t) | (lane == 4 * t + 1), turn(v, 4 * t - 126))
                    else:
                        row, at = (24 + t, 48 + 2 * t) if k < 6 else (36 + t, 72 + 2 * t)
                        top_ref[m, pl.ds(row, 1), :] = v[0:1]
                        bottom_ref[m, pl.ds(row, 1), :] = v[127:128]
                        if m == 0:
                            put(low_ref, lane == at + 1, turn(v, at + 1))
                        else:
                            put(high_ref, lane == at, turn(v, at - 127))
        written.append(pltpu.make_async_copy(planes.at[pl.ds(4 * k, 4)], out.at[pl.ds(t0, 4)], out_sems.at[k]))
        written[-1].start()
    for copy in written:
        copy.wait()


def start_side(x, t):
    lane = lanes_of(x.shape[0])
    return jnp.where((lane < 2) | (lane >= 126), turn(x, 126 - 4 * t), 0.0)


def other_side(x, at):
    lane = lanes_of(x.shape[0])
    return jnp.where((lane < 1) | (lane >= 127), turn(x, 127 - at), 0.0)


def rows_kernel(left_ref, right_ref, top_ref, bottom_ref, first_ref, last_ref, up_ref, down_ref):
    for part, patch, out, two, one in ((top_ref, first_ref, up_ref, 0, 0), (bottom_ref, last_ref, down_ref, 126, 127)):
        out[0:2, 0:40, :] = part[...]
        pair = left_ref[two : two + 2] + right_ref[two : two + 2]
        single = left_ref[one : one + 1] + right_ref[one : one + 1]
        for t in range(12):
            out[2, pl.ds(2 * t, 2), :] = start_side(pair, t)
            out[2, pl.ds(24 + t, 1), :] = other_side(single, 48 + 2 * t)
        for t in range(4):
            out[2, pl.ds(36 + t, 1), :] = other_side(single, 72 + 2 * t)
        for p in range(7):
            row, count = edge_rows(p)
            at = 0 if one == 0 else 8 - count
            for m in range(2):
                out[m, pl.ds(row, count), :] = patch[0, pl.ds((2 * p + m) * 8 + at, count), :]
            out[2, pl.ds(row, count), :] = beside(patch[0, pl.ds(112 + at, count), :], p)


def sweep_kernel(
    fs_hbm, fk_hbm, fm_hbm, recv_ref, left_ref, right_ref, above_ref, below_ref,
    chunk_ref, fine_hbm,
    ca, cb, xa, xb, kc, mc, rc, fa, fb, kf, mf, rf, fine_ref, sems, out_sems,
):
    own = pl.ds(TOP, PR)
    copies = [
        pltpu.make_async_copy(src, dst.at[:, pl.ds(0, 2), own, :], sems.at[n])
        for n, (src, dst) in enumerate(((fs_hbm, fa), (fk_hbm, kf), (fm_hbm, mf)))
    ]
    for copy in copies:
        copy.start()
    zero8 = jnp.zeros((8, 128), F32)
    for ref, count in ((ca, 3), (kc, 3), (fa, 12), (kf, 12), (mf, 4)):
        for t in range(count):
            for m in range(3):
                for r in (TOP - 8, TOP + PR):
                    ref[t, m, pl.ds(r, 8), :] = zero8
    for m in range(3):
        for r in (TOP - 8, TOP + PR):
            mc[m, pl.ds(r, 8), :] = zero8
    lane8 = lanes_of(8)

    def coarse(p):
        return (ca.at[p], kc.at[p - 3] if 3 <= p < 6 else None, mc)[0 if p < 3 else 1 if p < 6 else 2]

    for p in range(7):
        ref = coarse(p)
        for j in range(16):
            rows = pl.ds(TOP + 8 * j, 8)
            for m in range(2):
                ref[m, rows, :] = recv_ref[j, pl.ds((2 * p + m) * 8, 8), :]
            ref[2, rows, :] = beside(recv_ref[j, pl.ds(112, 8), :], p)
        row, count = edge_rows(p)
        for m in range(3):
            ref[m, pl.ds(TOP - count, count), :] = above_ref[m, pl.ds(row, count), :]
            ref[m, pl.ds(TOP + PR, count), :] = below_ref[m, pl.ds(row, count), :]
    both = left_ref[...] + right_ref[...]
    for t in range(12):
        fa[t, 2, own, :] = start_side(both, t)
        kf[t, 2, own, :] = other_side(both, 48 + 2 * t)
    for t in range(4):
        mf[t, 2, own, :] = other_side(both, 72 + 2 * t)
    for m in range(3):
        for t in range(12):
            fa[t, m, pl.ds(TOP - 2, 2), :] = above_ref[m, pl.ds(2 * t, 2), :]
            fa[t, m, pl.ds(TOP + PR, 2), :] = below_ref[m, pl.ds(2 * t, 2), :]
            kf[t, m, pl.ds(TOP - 1, 1), :] = above_ref[m, pl.ds(24 + t, 1), :]
            kf[t, m, pl.ds(TOP + PR, 1), :] = below_ref[m, pl.ds(24 + t, 1), :]
        for t in range(4):
            mf[t, m, pl.ds(TOP - 1, 1), :] = above_ref[m, pl.ds(36 + t, 1), :]
            mf[t, m, pl.ds(TOP + PR, 1), :] = below_ref[m, pl.ds(36 + t, 1), :]
    for copy in copies:
        copy.wait()

    at_start, at_end = lane8 == 0, lane8 == 127

    def before(x):
        turned = [turn(v, 1) for v in x]
        return [jnp.where(at_start, turned[m - 1], turned[m]) for m in range(len(x))]

    def after(x):
        turned = [turn(v, 127) for v in x]
        return [jnp.where(at_end, turned[(m + 1) % 3], turned[m]) for m in range(3)]

    def mix(x, k, r, c):
        west, east = before(c), after(c)
        for m in range(3):
            part = 0.375 * c[m]
            x[0, k, m, r, :] = part + 0.125 * west[m]
            x[1, k, m, r, :] = part + 0.125 * east[m]
            x[2, k, m, r, :] = west[m] + east[m]

    def ready(i, carry):
        r = pl.ds(pl.multiple_of(8 + 8 * i, 8), 8)
        for m in range(3):
            mu = mc[m, r, :]
            mc[m, r, :] = mu + 4.0
            rc[m, r, :] = jnp.where(mu > 0.0, 1.0 / (mu + 4.0), 0.0)
            for t in range(4):
                mu = mf[t, m, r, :]
                mf[t, m, r, :] = mu + 4.0
                rf[t, m, r, :] = jnp.where(mu > 0.0, 1.0 / (mu + 4.0), 0.0)
        for k in range(3):
            mix(xa, k, r, [ca[k, m, r, :] for m in range(3)])
        return carry

    lax.fori_loop(0, ROWS // 8 - 2, ready, 0)

    def step(r, c_old, x_old, f_old, store_c, store_f, tiles, sums):
        here, up, down = pl.ds(r, 8), pl.ds(r - 1, 8), pl.ds(r + 1, 8)
        totals = [zero8] * 4
        for k in range(3):
            f = [[[f_old[4 * k + 2 * p + q, m, here, :] for m in range(3)] for q in range(2)] for p in range(2)]
            far = [[(before, after)[q](f[p][1 - q]) for q in range(2)] for p in range(2)]
            new = []
            for m in range(tiles):
                for q in range(2):
                    mid = 3.0 * x_old[q, k, m, here, :]
                    for p in range(2):
                        t, side = 4 * k + 2 * p + q, (up, down)[p]
                        other = f_old[4 * k + 2 * (1 - p) + q, m, side, :]
                        near = (f[1 - p][q][m] + other) + (f[p][1 - q][m] + far[p][q][m])
                        s = (kf[t, m, here, :] + near) + (mid + x_old[q, k, m, side, :])
                        store_f(t, m, s * rf[2 * p + q, m, here, :])
                        if sums and m < 2:
                            res = s - mf[2 * p + q, m, here, :] * f[p][q][m]
                            totals[2 * p + q] = totals[2 * p + q] + res * res
                c = c_old[k, m, here, :]
                near = (c_old[k, m, up, :] + c_old[k, m, down, :]) + x_old[2, k, m, here, :]
                four = (f[0][0][m] + f[0][1][m]) + (f[1][0][m] + f[1][1][m])
                s = (kc[k, m, here, :] + 0.5 * four) + near
                new.append(s * rc[m, here, :])
                if sums and m < 2:
                    res = s - mc[m, here, :] * c
                    totals[k] = totals[k] + res * res
            store_c(k, new)
        return (totals[0] + totals[1]) + (totals[2] + totals[3])

    def sweep(c_old, x_old, f_old, c_new, x_new, f_new):
        def stores(r):
            rows = pl.ds(r, 8)

            def store_c(k, new):
                for m in range(3):
                    c_new[k, m, rows, :] = new[m]
                mix(x_new, k, rows, new)

            def store_f(t, m, v):
                f_new[t, m, rows, :] = v

            return store_c, store_f

        def body(i, total):
            r = pl.multiple_of(TOP + 8 * i, 8)
            return total + step(r, c_old, x_old, f_old, *stores(r), 3, True)

        total = lax.fori_loop(0, PR // 8, body, zero8)

        def edge(i, carry):
            r = pl.multiple_of(TOP - 8 + i * (PR + 8), 8)
            step(r, c_old, x_old, f_old, *stores(r), 3, False)
            return carry

        lax.fori_loop(0, 2, edge, 0)
        return total

    totals = [sweep(ca, xa, fa, cb, xb, fb), sweep(cb, xb, fb, ca, xa, fa)]

    def last(i, total):
        r = pl.multiple_of(TOP + 8 * i, 8)

        def store_c(k, new):
            for m in range(2):
                chunk_ref[i, pl.ds((2 * k + m) * 8, 8), :] = new[m]

        def store_f(t, m, v):
            fine_ref[t, m, pl.ds(pl.multiple_of(8 * i, 8), 8), :] = v

        return total + step(r, ca, xa, fa, store_c, store_f, 2, True)

    total, parts = zero8, 4
    written = []
    for n in range(parts):
        total = lax.fori_loop(n * PR // 8 // parts, (n + 1) * PR // 8 // parts, last, total)
        rows = pl.ds(n * PR // parts, PR // parts)
        written.append(pltpu.make_async_copy(fine_ref.at[:, :, rows], fine_hbm.at[:, :, rows], out_sems.at[n]))
        written[-1].start()
    totals.append(total)
    sums = 0.0625 * jnp.concatenate([jnp.sum(v, axis=0, keepdims=True) for v in totals] + [jnp.zeros((5, 128), F32)], axis=0)
    for j in range(16):
        chunk_ref[j, pl.ds(48, 8), :] = sums
    for copy in written:
        copy.wait()


def join_kernel(fine_hbm, out_hbm, fine_ref, block, in_sems, sems):
    reads = [
        pltpu.make_async_copy(fine_hbm.at[pl.ds(4 * k, 4)], fine_ref.at[pl.ds(4 * k, 4)], in_sems.at[k])
        for k in range(3)
    ]
    for copy in reads:
        copy.start()
    table = parity_table(False)
    copies = []
    for k in range(3):
        reads[k].wait()
        for m in range(2):
            for p in range(2):
                x = jnp.concatenate([fine_ref[4 * k + 2 * p + q, m, :, :] for q in range(2)], axis=1)
                y = permuted(x, table)
                for c in range(2):
                    block[k, 2 * m + c, pl.ds(p, PR, stride=2), :] = y[:, 128 * c : 128 * c + 128]
            for c in range(2 * m, 2 * m + 2):
                copy = pltpu.make_async_copy(
                    block.at[k, c], out_hbm.at[k, :, pl.ds(128 * c, 128)], sems.at[4 * k + c]
                )
                copy.start()
                copies.append(copy)
    for copy in copies:
        copy.wait()


def sum_kernel(recv_ref, out_ref):
    total = recv_ref[0]
    for j in range(1, 16):
        total = total + recv_ref[j]
    for i in range(8):
        out_ref[i] = total


def coarse_kernel(recv_ref, out_ref):
    for j in range(16):
        for k in range(3):
            for m in range(2):
                out_ref[k, :, pl.ds(256 * j + 128 * m, 128)] = recv_ref[j, pl.ds((2 * k + m) * 8, 8), :]


def on_device(fine_start, fine_known, fine_mu, coarse_start, coarse_known, coarse_mu):
    count_x, count_y = lax.axis_size(GX), lax.axis_size(GY)
    cell_total = 3.0 * (fine_mu.size + coarse_mu.size) * (count_x * count_y)
    chunk = pl.pallas_call(
        pack_kernel,
        out_shape=pltpu.VMEM((16, MAIN, 128), F32),
        in_specs=[HBM] * 3,
        out_specs=VMEM,
        scratch_shapes=[
            pltpu.VMEM(coarse_start.shape, F32),
            pltpu.VMEM(coarse_known.shape, F32),
            pltpu.VMEM(coarse_mu.shape, F32),
            pltpu.SemaphoreType.DMA((3,)),
        ],
        compiler_params=params(28672),
        cost_estimate=cost(2, 2e6),
        name="pack",
    )(*in_hbm(coarse_start, coarse_known, coarse_mu))
    recv = lax.all_to_all(chunk, GY, 0, 0, tiled=True)

    fs, fk, fm, low, high, top, bottom = pl.pallas_call(
        fine_kernel,
        out_shape=(
            *(pltpu.HBM((n, 2, PR, 128), F32) for n in (12, 12, 4)),
            *(pltpu.VMEM(shape, F32) for shape in ((PR, 128), (PR, 128), (2, 40, 128), (2, 40, 128))),
        ),
        in_specs=[HBM] * 3,
        out_specs=(HBM,) * 3 + (VMEM,) * 4,
        scratch_shapes=[
            pltpu.VMEM((7, 4, 2 * PR, 128), F32),
            pltpu.VMEM((28, 2, PR, 128), F32),
            pltpu.SemaphoreType.DMA((28,)),
            pltpu.SemaphoreType.DMA((7,)),
        ],
        compiler_params=params(28672),
        cost_estimate=cost(4, 7e6),
        name="fine",
    )(*in_hbm(fine_start, fine_known, fine_mu))

    def ahead(n):
        return [(i, i + 1) for i in range(n - 1)]

    def back(n):
        return [(i + 1, i) for i in range(n - 1)]

    left = lax.ppermute(high, GY, ahead(count_y))
    right = lax.ppermute(low, GY, back(count_y))
    up, down = pl.pallas_call(
        rows_kernel,
        grid=(1,),
        out_shape=(shaped(3, EDGE, 128),) * 2,
        in_specs=[pl.BlockSpec((PR, 128), lambda i: (0, 0))] * 2
        + [pl.BlockSpec((2, 40, 128), lambda i: (0, 0, 0))] * 2
        + [pl.BlockSpec((1, MAIN, 128), lambda i: (0, 0, 0)), pl.BlockSpec((1, MAIN, 128), lambda i: (15, 0, 0))],
        out_specs=(pl.BlockSpec((3, EDGE, 128), lambda i: (0, 0, 0)),) * 2,
        compiler_params=params(28672),
        cost_estimate=cost(1, 0.3e6),
        name="rows",
    )(left, right, top, bottom, recv, recv)
    above = lax.ppermute(down, GX, ahead(count_x))
    below = lax.ppermute(up, GX, back(count_x))

    chunk, fine = pl.pallas_call(
        sweep_kernel,
        out_shape=(shaped(16, 56, 128), pltpu.HBM((12, 2, PR, 128), F32)),
        in_specs=[HBM] * 3 + [VMEM] * 5,
        out_specs=(VMEM, HBM),
        scratch_shapes=[
            pltpu.VMEM((3, 3, ROWS, 128), F32),
            pltpu.VMEM((3, 3, ROWS, 128), F32),
            pltpu.VMEM((3, 3, 3, ROWS, 128), F32),
            pltpu.VMEM((3, 3, 3, ROWS, 128), F32),
            pltpu.VMEM((3, 3, ROWS, 128), F32),
            pltpu.VMEM((3, ROWS, 128), F32),
            pltpu.VMEM((3, ROWS, 128), F32),
            pltpu.VMEM((12, 3, ROWS, 128), F32),
            pltpu.VMEM((12, 3, ROWS, 128), F32),
            pltpu.VMEM((12, 3, ROWS, 128), F32),
            pltpu.VMEM((4, 3, ROWS, 128), F32),
            pltpu.VMEM((4, 3, ROWS, 128), F32),
            pltpu.VMEM((12, 2, PR, 128), F32),
            pltpu.SemaphoreType.DMA((3,)),
            pltpu.SemaphoreType.DMA((4,)),
        ],
        compiler_params=params(28672),
        cost_estimate=cost(8, 7e6),
        name="sweeps",
    )(*in_hbm(fs, fk, fm), recv, left, right, above, below)
    out = lax.all_to_all(chunk, GY, 0, 0, tiled=True)

    fine_ghost = pl.pallas_call(
        join_kernel,
        out_shape=shaped(*fine_start.shape),
        in_specs=[HBM],
        out_specs=HBM,
        scratch_shapes=[
            pltpu.VMEM((12, 2, PR, 128), F32),
            pltpu.VMEM((3, 4, 2 * PR, 128), F32),
            pltpu.SemaphoreType.DMA((3,)),
            pltpu.SemaphoreType.DMA((12,)),
        ],
        compiler_params=params(28672),
        cost_estimate=cost(2, 3e6),
        name="join",
    )(*in_hbm(fine))
    sums = pl.pallas_call(
        sum_kernel,
        grid=(1,),
        out_shape=shaped(8, 8, 128),
        in_specs=[pl.BlockSpec((16, 8, 128), lambda i: (0, 6, 0))],
        out_specs=pl.BlockSpec((8, 8, 128), lambda i: (0, 0, 0)),
        compiler_params=params(28672),
        cost_estimate=cost(1, 0.1e6),
        name="sums",
    )(out)
    sums = lax.all_to_all(sums, GX, 0, 0, tiled=True)
    coarse_ghost = pl.pallas_call(
        coarse_kernel,
        out_shape=shaped(*coarse_start.shape),
        in_specs=[VMEM],
        out_specs=VMEM,
        compiler_params=params(28672),
        cost_estimate=cost(1, 0.8e6),
        name="coarse",
    )(out)
    norms = jnp.sqrt(jnp.sum(sums[:, :ITERS, :], axis=(0, 2)) / cell_total)
    return fine_ghost, coarse_ghost, norms


def solution(mesh):
    fine, coarse = P(None, GX, GY), P(None, BOTH, None)
    return jax.shard_map(
        on_device,
        mesh=mesh,
        in_specs=(fine, fine, P(GX, GY), coarse, coarse, P(BOTH, None)),
        out_specs=(fine, coarse, P()),
        check_vma=False,
    )
```

time: 104 us -> 79.6 us (0.77)
  waiting for transfers between devices: 19.7 us -> 10 us
  Pallas kernels: 33 us -> 25.1 us
  local copies, waits for them, and re-layouts: 2.43 us -> 0 us
  blocking collectives: 17.5 us -> 15.4 us
  starting transfers between devices: 28.9 us -> 27.2 us
    ppermute x1 -> x0, starting transfers between devices: 9.48 us -> none  [on_device(): edge = lax.ppermute(edge, BOTH, pairs + [(b, a) for a, b in pairs])]
    ppermute x1 -> x0, waiting for transfers between devices: 7.82 us -> none  [on_device(): edge = lax.ppermute(edge, BOTH, pairs + [(b, a) for a, b in pairs])]
    pallas_call x5 -> x4, Pallas kernels: 26.7 us -> 20.7 us  [the longest x1 12.7 us: on_device(): pl.pallas_call(sweep_kernel, out_shape=(shaped(16, 56, 128), pltpu.HBM((1...]
    all_to_all x1, starting transfers between devices: 4.02 us -> 8.6 us  [on_device(): recv = lax.all_to_all(chunk, GY, 0, 0, tiled=True)]
    ppermute x1, waiting for transfers between devices: 6.49 us -> 3.67 us  [on_device(): left = lax.ppermute(high, GY, ahead(count_y))]
    unnamed x12 -> x0, local copies, waits for them, and re-layouts: 2.43 us -> none
    all_to_all x1, blocking collectives: 17.5 us -> 15.4 us  [on_device(): out = lax.all_to_all(chunk, GY, 0, 0, tiled=True)]
    ppermute x1, starting transfers between devices: 4.05 us -> 5.67 us  [on_device(): above = lax.ppermute(down, GX, ahead(count_x))]
  transfers between devices with their start and end apart: 7 -> 6, of which waited for: 4 -> 4; matrix products, arithmetic and copies ran while one was open for 0% -> 0% of each run, Pallas kernels for 12% -> 12%
where the time goes in v1:
time: 79.6 us; the launch traced here: 79.1 us
  starting transfers between devices  27.2 us (34%)
  Pallas kernels  25.1 us (32%)
  blocking collectives  15.4 us (19%)
  waiting for transfers between devices  10 us (13%)
    all_to_all x1, blocking collectives, on_device(): out = lax.all_to_all(chunk, GY, 0, 0, tiled=True)  15.4 us
    pallas_call x1, Pallas kernels, on_device(): pl.pallas_call(sweep_kernel, out_shape=(shaped(16, 56, 128), pltpu.HBM((1...  12.7 us
    all_to_all x1, starting transfers between devices, on_device(): recv = lax.all_to_all(chunk, GY, 0, 0, tiled=True)  8.6 us
    all_to_all x1, starting transfers between devices, on_device(): sums = lax.all_to_all(sums, GX, 0, 0, tiled=True)  6.4 us
    ppermute x1, starting transfers between devices, on_device(): above = lax.ppermute(down, GX, ahead(count_x))  5.67 us
    pallas_call x1, Pallas kernels, on_device(): pl.pallas_call(fine_kernel, out_shape=(*(pltpu.HBM((n, 2, PR, 128), F32)...  5.56 us
    ppermute x1, waiting for transfers between devices, on_device(): below = lax.ppermute(up, GX, back(count_x))  4 us
    ppermute x1, waiting for transfers between devices, on_device(): left = lax.ppermute(high, GY, ahead(count_y))  3.67 us
  transfers between devices with their start and end apart: 6, of which 4 were waited for; matrix products, arithmetic and copies ran while one was open for 0% of the time, Pallas kernels for 12%

profile of v1, /device:TPU:1, one launch (start us, length us, event | category | flops | bytes accessed | tf_op | source)
XLA Modules:
  0.0 79.1 jit_solution(17595052462858744467)
XLA Ops:
  0.6 2.3 %pack.1 = f32[16,120,128]{2,1,0:T(8,128)} custom-call(f32[3,8,4096]{2,1,0:T(8,128)} %start_hbm.3, f32[3,8,4096]{2,1,0:T(8,128)} %known_hbm.3, f32[8,4096]{1,0:T(8,128)} %mu_hbm.3), custom_call_target="tpu_custom_call" | custom-call | flops 14000000 | bytes 2000000 | tf_op jit(solution)/shard_map/pack/pallas_call | solution.py:423
  2.9 8.6 %all-to-all-start = ((f32[16,120,128]{2,1,0:T(8,128)}), f32[16,120,128]{2,1,0:T(8,128)S(1)}, u32[]{:S(2)}, u32[]{:S(2)}) async-start(f32[16,120,128]{2,1,0:T(8,128)} %pack.1), calls=%async_computation | async-start | bytes 1966080 | tf_op jit(solution)/shard_map/all_to_all | solution.py:438
  11.5 5.6 %fine.1 = (f32[12,2,128,128]{3,2,1,0:T(8,128)}, f32[12,2,128,128]{3,2,1,0:T(8,128)}, f32[4,2,128,128]{3,2,1,0:T(8,128)}, f32[128,128]{1,0:T(8,128)S(1)}, f32[128...) custom-call(f32[3,256,512]{2,1,0:T(8,128)} %start_hbm.2, f32[3,256,512]{2,1,0:T(8,128)} %known_hbm.2, ...), custom_call_target="tpu_custom_call" | custom-call | flops 28000000 | bytes 7000000 | tf_op jit(solution)/shard_map/fine/pallas_call | solution.py:440
  17.1 3.3 %collective-permute-start = (f32[128,128]{1,0:T(8,128)S(1)}, f32[128,128]{1,0:T(8,128)S(1)}, u32[]{:S(2)}, u32[]{:S(2)}) collective-permute-start(f32[128,128]{1,0:T(8,128)S(1)} %get-tuple-element.17), channel_id=1, source_target_pairs={{0,1},{1,2},{2,3},{3,4},{4,5},{5,6},{6,7},{7,8},{8,9},{9,10},{10,1... | collective-permute-start | bytes 196616 | tf_op jit(solution)/shard_map/ppermute | solution.py:465
  20.4 1.3 %collective-permute-start.1 = (f32[128,128]{1,0:T(8,128)S(1)}, f32[128,128]{1,0:T(8,128)S(1)}, u32[]{:S(2)}, u32[]{:S(2)}) collective-permute-start(f32[128,128]{1,0:T(8,128)S(1)} %get-tuple-element.18), channel_id=1, source_target_pairs={{1,0},{2,1},{3,2},{4,3},{5,4},{6,5},{7,6},{8,7},{9,8},{10,9},{11,1... | collective-permute-start | bytes 196616 | tf_op jit(solution)/shard_map/ppermute | solution.py:466
  21.7 3.7 %collective-permute-done.left_ref = f32[128,128]{1,0:T(8,128)S(1)} collective-permute-done((f32[128,128]{1,0:T(8,128)S(1)}, f32[128,128]{1,0:T(8,128)S(1)}, u32[]{:S(2)}, u32[]{:S(2)}) %collective-permute-start) | collective-permute-done | bytes 65568 | tf_op jit(solution)/shard_map/ppermute | solution.py:465
  25.4 1.5 %collective-permute-done.1.right_ref = f32[128,128]{1,0:T(8,128)S(1)} collective-permute-done((f32[128,128]{1,0:T(8,128)S(1)}, f32[128,128]{1,0:T(8,128)S(1)}, u32[]{:S(2)}, u32[]{:S(2)}) %collective-permute-start.1) | collective-permute-done | bytes 65568 | tf_op jit(solution)/shard_map/ppermute | solution.py:466
  26.8 0.0 all-to-all-done.first_ref.last_ref.recv_ref
  26.8 0.1 rows.1
  27.0 5.7 %collective-permute-start.2 = (f32[3,64,128]{2,1,0:T(8,128)S(1)}, f32[3,64,128]{2,1,0:T(8,128)S(1)}, u32[]{:S(2)}, u32[]{:S(2)}) collective-permute-start(f32[3,64,128]{2,1,0:T(8,128)S(1)} %get-tuple-element.21), channel_id=1, source_target_pairs={{0,16},{16,32},{32,48},{48,64},{64,80},{80,96},{96,112},{1,17},{17... | collective-permute-start | bytes 294920 | tf_op jit(solution)/shard_map/ppermute | solution.py:479
  32.6 1.9 %collective-permute-start.3 = (f32[3,64,128]{2,1,0:T(8,128)S(1)}, f32[3,64,128]{2,1,0:T(8,128)S(1)}, u32[]{:S(2)}, u32[]{:S(2)}) collective-permute-start(f32[3,64,128]{2,1,0:T(8,128)S(1)} %get-tuple-element.22), channel_id=1, source_target_pairs={{16,0},{32,16},{48,32},{64,48},{80,64},{96,80},{112,96},{17,1},{33... | collective-permute-start | bytes 294920 | tf_op jit(solution)/shard_map/ppermute | solution.py:480
  34.6 0.0 collective-permute-done.2.above_ref
  34.6 4.0 %collective-permute-done.3.below_ref = f32[3,64,128]{2,1,0:T(8,128)S(1)} collective-permute-done((f32[3,64,128]{2,1,0:T(8,128)S(1)}, f32[3,64,128]{2,1,0:T(8,128)S(1)}, u32[]{:S(2)}, u32[]{:S(2)}) %collective-permute-start.3) | collective-permute-done | bytes 98336 | tf_op jit(solution)/shard_map/ppermute | solution.py:480
  38.6 12.7 %sweeps.1 = (f32[16,56,128]{2,1,0:T(8,128)S(1)}, f32[12,2,128,128]{3,2,1,0:T(8,128)}) custom-call(f32[12,2,128,128]{3,2,1,0:T(8,128)} %get-tuple-element.14.fs_hbm, f32[12,2,128,128]{3,2,1,0:T(8,128)} %get-tuple-element.15.fk_hbm, f32[4,2,128,128]{3,2,1,0:T(8,128)} %get-tuple-element.16.fm_hbm, f32[16,120,128]{2,1,0:T(8,128)S(1)} %all-to-all-done.first_ref.last_ref.recv_ref, ...), custom_call_target="tpu_custom_call" | custom-call | flops 56000000 | bytes 7000000 | tf_op jit(solution)/shard_map/sweeps/pallas_call | solution.py:482
  51.3 15.4 %all_to_all.15.recv_ref = f32[16,56,128]{2,1,0:T(8,128)S(1)} all-to-all(f32[16,56,128]{2,1,0:T(8,128)S(1)} %get-tuple-element.24), channel_id=1, replica_groups=mesh['gx'=8,'gy'=16] {'gy'}, dimensions={0} | all-to-all | bytes 917504 | tf_op jit(solution)/shard_map/all_to_all | solution.py:508
  66.8 0.6 sums.1
  67.4 6.4 %all-to-all-start.2 = ((f32[8,8,128]{2,1,0:T(8,128)}), f32[8,8,128]{2,1,0:T(8,128)S(1)}, u32[]{:S(2)}, u32[]{:S(2)}) async-start(f32[8,8,128]{2,1,0:T(8,128)} %sums.1), calls=%async_computation.2 | async-start | bytes 65536 | tf_op jit(solution)/shard_map/all_to_all | solution.py:535
  73.8 3.0 %join.1 = f32[3,256,512]{2,1,0:T(8,128)} custom-call(f32[12,2,128,128]{3,2,1,0:T(8,128)} %get-tuple-element.23.fine_hbm), custom_call_target="tpu_custom_call" | custom-call | flops 14000000 | bytes 3000000 | tf_op jit(solution)/shard_map/join/pallas_call | solution.py:510
  76.8 0.8 coarse.1
  77.6 0.9 %all-to-all-done.2 = f32[8,8,128]{2,1,0:T(8,128)S(1)} async-done(((f32[8,8,128]{2,1,0:T(8,128)}), f32[8,8,128]{2,1,0:T(8,128)S(1)}, u32[]{:S(2)}, u32[]{:S(2)}) %all-to-all-start.2) | async-done | bytes 32800 | tf_op jit(solution)/shard_map/all_to_all | solution.py:535
  78.5 0.1 slice_reduce_fusion
  78.6 0.5 multiply_sqrt_fusion
Async XLA Ops:
  2.9 23.9 %all-to-all-start = ((f32[16,120,128]{2,1,0:T(8,128)}), f32[16,120,128]{2,1,0:T(8,128)S(1)}, u32[]{:S(2)}, u32[]{:S(2)}) async-start(f32[16,120,128]{2,1,0:T(8,128)} %pack.1), calls=%async_computation | async-start | bytes 1966080 | tf_op jit(solution)/shard_map/all_to_all | solution.py:438
  17.1 8.3 %collective-permute-start = (f32[128,128]{1,0:T(8,128)S(1)}, f32[128,128]{1,0:T(8,128)S(1)}, u32[]{:S(2)}, u32[]{:S(2)}) collective-permute-start(f32[128,128]{1,0:T(8,128)S(1)} %get-tuple-element.17), channel_id=1, source_target_pairs={{0,1},{1,2},{2,3},{3,4},{4,5},{5,6},{6,7},{7,8},{8,9},{9,10},{10,1... | collective-permute-start | bytes 196616 | tf_op jit(solution)/shard_map/ppermute | solution.py:465
  20.4 6.4 %collective-permute-start.1 = (f32[128,128]{1,0:T(8,128)S(1)}, f32[128,128]{1,0:T(8,128)S(1)}, u32[]{:S(2)}, u32[]{:S(2)}) collective-permute-start(f32[128,128]{1,0:T(8,128)S(1)} %get-tuple-element.18), channel_id=1, source_target_pairs={{1,0},{2,1},{3,2},{4,3},{5,4},{6,5},{7,6},{8,7},{9,8},{10,9},{11,1... | collective-permute-start | bytes 196616 | tf_op jit(solution)/shard_map/ppermute | solution.py:466
  27.0 7.6 %collective-permute-start.2 = (f32[3,64,128]{2,1,0:T(8,128)S(1)}, f32[3,64,128]{2,1,0:T(8,128)S(1)}, u32[]{:S(2)}, u32[]{:S(2)}) collective-permute-start(f32[3,64,128]{2,1,0:T(8,128)S(1)} %get-tuple-element.21), channel_id=1, source_target_pairs={{0,16},{16,32},{32,48},{48,64},{64,80},{80,96},{96,112},{1,17},{17... | collective-permute-start | bytes 294920 | tf_op jit(solution)/shard_map/ppermute | solution.py:479
  32.6 5.9 %collective-permute-start.3 = (f32[3,64,128]{2,1,0:T(8,128)S(1)}, f32[3,64,128]{2,1,0:T(8,128)S(1)}, u32[]{:S(2)}, u32[]{:S(2)}) collective-permute-start(f32[3,64,128]{2,1,0:T(8,128)S(1)} %get-tuple-element.22), channel_id=1, source_target_pairs={{16,0},{32,16},{48,32},{64,48},{80,64},{96,80},{112,96},{17,1},{33... | collective-permute-start | bytes 294920 | tf_op jit(solution)/shard_map/ppermute | solution.py:480
  67.4 11.1 %all-to-all-start.2 = ((f32[8,8,128]{2,1,0:T(8,128)}), f32[8,8,128]{2,1,0:T(8,128)S(1)}, u32[]{:S(2)}, u32[]{:S(2)}) async-start(f32[8,8,128]{2,1,0:T(8,128)} %sums.1), calls=%async_computation.2 | async-start | bytes 65536 | tf_op jit(solution)/shard_map/all_to_all | solution.py:535

commit v2 on v1

--- a/solution.py
+++ b/solution.py
@@ -10,7 +10,7 @@
 BOTH = (GX, GY)
 PR = 128
 TOP = 16
-ROWS = PR + 2 * TOP
+ROWS = PR + 40
 F32 = jnp.float32
 BF16 = jnp.bfloat16
 VMEM = pl.BlockSpec(memory_space=pltpu.VMEM)
@@ -21,7 +21,7 @@
     return jax.ShapeDtypeStruct(shape, F32)
 
 
-ALL_KIB = 65472
+GRANT_KIB = 36864
 
 
 def params(kib):
@@ -201,13 +201,13 @@
 
 def sweep_kernel(
     fs_hbm, fk_hbm, fm_hbm, recv_ref, left_ref, right_ref, above_ref, below_ref,
-    chunk_ref, fine_hbm,
-    ca, cb, xa, xb, kc, mc, rc, fa, fb, kf, mf, rf, fine_ref, sems, out_sems,
+    chunk_ref, fine_ref,
+    ca, cb, xa, xb, kc, mc, rc, fa, fb, kf, mf, rf, sems,
 ):
     own = pl.ds(TOP, PR)
     copies = [
         pltpu.make_async_copy(src, dst.at[:, pl.ds(0, 2), own, :], sems.at[n])
-        for n, (src, dst) in enumerate(((fs_hbm, fa), (fk_hbm, kf), (fm_hbm, mf)))
+        for n, (src, dst) in enumerate(((fm_hbm, mf), (fs_hbm, fa), (fk_hbm, kf)))
     ]
     for copy in copies:
         copy.start()
@@ -251,8 +251,7 @@
         for t in range(4):
             mf[t, m, pl.ds(TOP - 1, 1), :] = above_ref[m, pl.ds(36 + t, 1), :]
             mf[t, m, pl.ds(TOP + PR, 1), :] = below_ref[m, pl.ds(36 + t, 1), :]
-    for copy in copies:
-        copy.wait()
+    copies[0].wait()
 
     at_start, at_end = lane8 == 0, lane8 == 127
 
@@ -286,7 +285,9 @@
             mix(xa, k, r, [ca[k, m, r, :] for m in range(3)])
         return carry
 
-    lax.fori_loop(0, ROWS // 8 - 2, ready, 0)
+    lax.fori_loop(0, PR // 8 + 2, ready, 0, unroll=6)
+    for copy in copies[1:]:
+        copy.wait()
 
     def step(r, c_old, x_old, f_old, store_c, store_f, tiles, sums):
         here, up, down = pl.ds(r, 8), pl.ds(r - 1, 8), pl.ds(r + 1, 8)
@@ -336,14 +337,14 @@
             r = pl.multiple_of(TOP + 8 * i, 8)
             return total + step(r, c_old, x_old, f_old, *stores(r), 3, True)
 
-        total = lax.fori_loop(0, PR // 8, body, zero8)
+        total = lax.fori_loop(0, PR // 8, body, zero8, unroll=4)
 
         def edge(i, carry):
             r = pl.multiple_of(TOP - 8 + i * (PR + 8), 8)
             step(r, c_old, x_old, f_old, *stores(r), 3, False)
             return carry
 
-        lax.fori_loop(0, 2, edge, 0)
+        lax.fori_loop(0, 2, edge, 0, unroll=True)
         return total
 
     totals = [sweep(ca, xa, fa, cb, xb, fb), sweep(cb, xb, fb, ca, xa, fa)]
@@ -360,32 +361,16 @@
 
         return total + step(r, ca, xa, fa, store_c, store_f, 2, True)
 
-    total, parts = zero8, 4
-    written = []
-    for n in range(parts):
-        total = lax.fori_loop(n * PR // 8 // parts, (n + 1) * PR // 8 // parts, last, total)
-        rows = pl.ds(n * PR // parts, PR // parts)
-        written.append(pltpu.make_async_copy(fine_ref.at[:, :, rows], fine_hbm.at[:, :, rows], out_sems.at[n]))
-        written[-1].start()
-    totals.append(total)
+    totals.append(lax.fori_loop(0, PR // 8, last, zero8, unroll=4))
     sums = 0.0625 * jnp.concatenate([jnp.sum(v, axis=0, keepdims=True) for v in totals] + [jnp.zeros((5, 128), F32)], axis=0)
     for j in range(16):
         chunk_ref[j, pl.ds(48, 8), :] = sums
-    for copy in written:
-        copy.wait()
-
-
-def join_kernel(fine_hbm, out_hbm, fine_ref, block, in_sems, sems):
-    reads = [
-        pltpu.make_async_copy(fine_hbm.at[pl.ds(4 * k, 4)], fine_ref.at[pl.ds(4 * k, 4)], in_sems.at[k])
-        for k in range(3)
-    ]
-    for copy in reads:
-        copy.start()
+
+
+def join_kernel(fine_ref, out_hbm, block, sems):
     table = parity_table(False)
     copies = []
     for k in range(3):
-        reads[k].wait()
         for m in range(2):
             for p in range(2):
                 x = jnp.concatenate([fine_ref[4 * k + 2 * p + q, m, :, :] for q in range(2)], axis=1)
@@ -431,7 +416,7 @@
             pltpu.VMEM(coarse_mu.shape, F32),
             pltpu.SemaphoreType.DMA((3,)),
         ],
-        compiler_params=params(28672),
+        compiler_params=params(GRANT_KIB),
         cost_estimate=cost(2, 2e6),
         name="pack",
     )(*in_hbm(coarse_start, coarse_known, coarse_mu))
@@ -451,7 +436,7 @@
             pltpu.SemaphoreType.DMA((28,)),
             pltpu.SemaphoreType.DMA((7,)),
         ],
-        compiler_params=params(28672),
+        compiler_params=params(GRANT_KIB),
         cost_estimate=cost(4, 7e6),
         name="fine",
     )(*in_hbm(fine_start, fine_known, fine_mu))
@@ -472,7 +457,7 @@
         + [pl.BlockSpec((2, 40, 128), lambda i: (0, 0, 0))] * 2
         + [pl.BlockSpec((1, MAIN, 128), lambda i: (0, 0, 0)), pl.BlockSpec((1, MAIN, 128), lambda i: (15, 0, 0))],
         out_specs=(pl.BlockSpec((3, EDGE, 128), lambda i: (0, 0, 0)),) * 2,
-        compiler_params=params(28672),
+        compiler_params=params(GRANT_KIB),
         cost_estimate=cost(1, 0.3e6),
         name="rows",
     )(left, right, top, bottom, recv, recv)
@@ -481,9 +466,9 @@
 
     chunk, fine = pl.pallas_call(
         sweep_kernel,
-        out_shape=(shaped(16, 56, 128), pltpu.HBM((12, 2, PR, 128), F32)),
+        out_shape=(pltpu.VMEM((16, 56, 128), F32), pltpu.VMEM((12, 2, PR, 128), F32)),
         in_specs=[HBM] * 3 + [VMEM] * 5,
-        out_specs=(VMEM, HBM),
+        out_specs=(VMEM, VMEM),
         scratch_shapes=[
             pltpu.VMEM((3, 3, ROWS, 128), F32),
             pltpu.VMEM((3, 3, ROWS, 128), F32),
@@ -497,11 +482,9 @@
             pltpu.VMEM((12, 3, ROWS, 128), F32),
             pltpu.VMEM((4, 3, ROWS, 128), F32),
             pltpu.VMEM((4, 3, ROWS, 128), F32),
-            pltpu.VMEM((12, 2, PR, 128), F32),
             pltpu.SemaphoreType.DMA((3,)),
-            pltpu.SemaphoreType.DMA((4,)),
         ],
-        compiler_params=params(28672),
+        compiler_params=params(GRANT_KIB),
         cost_estimate=cost(8, 7e6),
         name="sweeps",
     )(*in_hbm(fs, fk, fm), recv, left, right, above, below)
@@ -510,25 +493,23 @@
     fine_ghost = pl.pallas_call(
         join_kernel,
         out_shape=shaped(*fine_start.shape),
-        in_specs=[HBM],
+        in_specs=[VMEM],
         out_specs=HBM,
         scratch_shapes=[
-            pltpu.VMEM((12, 2, PR, 128), F32),
             pltpu.VMEM((3, 4, 2 * PR, 128), F32),
-            pltpu.SemaphoreType.DMA((3,)),
             pltpu.SemaphoreType.DMA((12,)),
         ],
-        compiler_params=params(28672),
+        compiler_params=params(GRANT_KIB),
         cost_estimate=cost(2, 3e6),
         name="join",
-    )(*in_hbm(fine))
+    )(fine)
     sums = pl.pallas_call(
         sum_kernel,
         grid=(1,),
-        out_shape=shaped(8, 8, 128),
+        out_shape=pltpu.VMEM((8, 8, 128), F32),
         in_specs=[pl.BlockSpec((16, 8, 128), lambda i: (0, 6, 0))],
         out_specs=pl.BlockSpec((8, 8, 128), lambda i: (0, 0, 0)),
-        compiler_params=params(28672),
+        compiler_params=params(GRANT_KIB),
         cost_estimate=cost(1, 0.1e6),
         name="sums",
     )(out)
@@ -538,7 +519,7 @@
         out_shape=shaped(*coarse_start.shape),
         in_specs=[VMEM],
         out_specs=VMEM,
-        compiler_params=params(28672),
+        compiler_params=params(GRANT_KIB),
         cost_estimate=cost(1, 0.8e6),
         name="coarse",
     )(out)

time: 79.6 us -> 74.7 us (0.938)
  Pallas kernels: 25.1 us -> 18.9 us
  waiting for transfers between devices: 10 us -> 11.4 us
    pallas_call x2, Pallas kernels: 13.3 us -> 8.54 us  [the longest x1 7.92 us: on_device(): pl.pallas_call(sweep_kernel, out_shape=(pltpu.VMEM((16, 56, 128), F32), p...]
    pallas_call x1, Pallas kernels: 3.04 us -> 1.63 us  [on_device(): pl.pallas_call(join_kernel, out_shape=shaped(*fine_start.shape), in_specs...]
    all_to_all x1, waiting for transfers between devices: 0.9 us -> 2.31 us  [on_device(): sums = lax.all_to_all(sums, GX, 0, 0, tiled=True)]
  transfers between devices with their start and end apart: 6 -> 6, of which waited for: 4 -> 4; matrix products, arithmetic and copies ran while one was open for 0% -> 0% of each run, Pallas kernels for 12% -> 11%
where the time goes in v2:
time: 74.7 us; the launch traced here: 74.3 us
  starting transfers between devices  27.2 us (36%)
  Pallas kernels  18.9 us (25%)
  blocking collectives  15.4 us (21%)
  waiting for transfers between devices  11.4 us (15%)
    all_to_all x1, blocking collectives, on_device(): out = lax.all_to_all(chunk, GY, 0, 0, tiled=True)  15.4 us
    all_to_all x1, starting transfers between devices, on_device(): recv = lax.all_to_all(chunk, GY, 0, 0, tiled=True)  8.6 us
    pallas_call x1, Pallas kernels, on_device(): pl.pallas_call(sweep_kernel, out_shape=(pltpu.VMEM((16, 56, 128), F32), p...  7.92 us
    all_to_all x1, starting transfers between devices, on_device(): sums = lax.all_to_all(sums, GX, 0, 0, tiled=True)  6.4 us
    ppermute x1, starting transfers between devices, on_device(): above = lax.ppermute(down, GX, ahead(count_x))  5.68 us
    pallas_call x1, Pallas kernels, on_device(): pl.pallas_call(fine_kernel, out_shape=(*(pltpu.HBM((n, 2, PR, 128), F32)...  5.56 us
    ppermute x1, waiting for transfers between devices, on_device(): below = lax.ppermute(up, GX, back(count_x))  4 us
    ppermute x1, waiting for transfers between devices, on_device(): left = lax.ppermute(high, GY, ahead(count_y))  3.66 us
  transfers between devices with their start and end apart: 6, of which 4 were waited for; matrix products, arithmetic and copies ran while one was open for 0% of the time, Pallas kernels for 11%

profile of v2, /device:TPU:1, one launch (start us, length us, event | category | flops | bytes accessed | tf_op | source)
XLA Modules:
  0.0 74.3 jit_solution(1499961226638477484)
XLA Ops:
  0.6 2.3 %pack.1 = f32[16,120,128]{2,1,0:T(8,128)} custom-call(f32[3,8,4096]{2,1,0:T(8,128)} %start_hbm.3, f32[3,8,4096]{2,1,0:T(8,128)} %known_hbm.3, f32[8,4096]{1,0:T(8,128)} %mu_hbm.3), custom_call_target="tpu_custom_call" | custom-call | flops 14000000 | bytes 2000000 | tf_op jit(solution)/shard_map/pack/pallas_call | solution.py:408
  2.9 8.6 %all-to-all-start = ((f32[16,120,128]{2,1,0:T(8,128)}), f32[16,120,128]{2,1,0:T(8,128)S(1)}, u32[]{:S(2)}, u32[]{:S(2)}) async-start(f32[16,120,128]{2,1,0:T(8,128)} %pack.1), calls=%async_computation | async-start | bytes 1966080 | tf_op jit(solution)/shard_map/all_to_all | solution.py:423
  11.5 5.6 %fine.1 = (f32[12,2,128,128]{3,2,1,0:T(8,128)}, f32[12,2,128,128]{3,2,1,0:T(8,128)}, f32[4,2,128,128]{3,2,1,0:T(8,128)}, f32[128,128]{1,0:T(8,128)S(1)}, f32[128...) custom-call(f32[3,256,512]{2,1,0:T(8,128)} %start_hbm.2, f32[3,256,512]{2,1,0:T(8,128)} %known_hbm.2, ...), custom_call_target="tpu_custom_call" | custom-call | flops 28000000 | bytes 7000000 | tf_op jit(solution)/shard_map/fine/pallas_call | solution.py:425
  17.1 3.3 %collective-permute-start = (f32[128,128]{1,0:T(8,128)S(1)}, f32[128,128]{1,0:T(8,128)S(1)}, u32[]{:S(2)}, u32[]{:S(2)}) collective-permute-start(f32[128,128]{1,0:T(8,128)S(1)} %get-tuple-element.17), channel_id=1, source_target_pairs={{0,1},{1,2},{2,3},{3,4},{4,5},{5,6},{6,7},{7,8},{8,9},{9,10},{10,1... | collective-permute-start | bytes 196616 | tf_op jit(solution)/shard_map/ppermute | solution.py:450
  20.4 1.3 %collective-permute-start.1 = (f32[128,128]{1,0:T(8,128)S(1)}, f32[128,128]{1,0:T(8,128)S(1)}, u32[]{:S(2)}, u32[]{:S(2)}) collective-permute-start(f32[128,128]{1,0:T(8,128)S(1)} %get-tuple-element.18), channel_id=1, source_target_pairs={{1,0},{2,1},{3,2},{4,3},{5,4},{6,5},{7,6},{8,7},{9,8},{10,9},{11,1... | collective-permute-start | bytes 196616 | tf_op jit(solution)/shard_map/ppermute | solution.py:451
  21.7 3.7 %collective-permute-done.left_ref = f32[128,128]{1,0:T(8,128)S(1)} collective-permute-done((f32[128,128]{1,0:T(8,128)S(1)}, f32[128,128]{1,0:T(8,128)S(1)}, u32[]{:S(2)}, u32[]{:S(2)}) %collective-permute-start) | collective-permute-done | bytes 65568 | tf_op jit(solution)/shard_map/ppermute | solution.py:450
  25.4 1.5 %collective-permute-done.1.right_ref = f32[128,128]{1,0:T(8,128)S(1)} collective-permute-done((f32[128,128]{1,0:T(8,128)S(1)}, f32[128,128]{1,0:T(8,128)S(1)}, u32[]{:S(2)}, u32[]{:S(2)}) %collective-permute-start.1) | collective-permute-done | bytes 65568 | tf_op jit(solution)/shard_map/ppermute | solution.py:451
  26.8 0.0 all-to-all-done.first_ref.last_ref.recv_ref
  26.8 0.1 rows.1
  27.0 5.7 %collective-permute-start.2 = (f32[3,64,128]{2,1,0:T(8,128)S(1)}, f32[3,64,128]{2,1,0:T(8,128)S(1)}, u32[]{:S(2)}, u32[]{:S(2)}) collective-permute-start(f32[3,64,128]{2,1,0:T(8,128)S(1)} %get-tuple-element.21), channel_id=1, source_target_pairs={{0,16},{16,32},{32,48},{48,64},{64,80},{80,96},{96,112},{1,17},{17... | collective-permute-start | bytes 294920 | tf_op jit(solution)/shard_map/ppermute | solution.py:464
  32.6 1.9 %collective-permute-start.3 = (f32[3,64,128]{2,1,0:T(8,128)S(1)}, f32[3,64,128]{2,1,0:T(8,128)S(1)}, u32[]{:S(2)}, u32[]{:S(2)}) collective-permute-start(f32[3,64,128]{2,1,0:T(8,128)S(1)} %get-tuple-element.22), channel_id=1, source_target_pairs={{16,0},{32,16},{48,32},{64,48},{80,64},{96,80},{112,96},{17,1},{33... | collective-permute-start | bytes 294920 | tf_op jit(solution)/shard_map/ppermute | solution.py:465
  34.6 0.0 collective-permute-done.2.above_ref
  34.6 4.0 %collective-permute-done.3.below_ref = f32[3,64,128]{2,1,0:T(8,128)S(1)} collective-permute-done((f32[3,64,128]{2,1,0:T(8,128)S(1)}, f32[3,64,128]{2,1,0:T(8,128)S(1)}, u32[]{:S(2)}, u32[]{:S(2)}) %collective-permute-start.3) | collective-permute-done | bytes 98336 | tf_op jit(solution)/shard_map/ppermute | solution.py:465
  38.6 7.9 %sweeps.1 = (f32[16,56,128]{2,1,0:T(8,128)S(1)}, f32[12,2,128,128]{3,2,1,0:T(8,128)S(1)}) custom-call(f32[12,2,128,128]{3,2,1,0:T(8,128)} %get-tuple-element.14.fs_hbm, f32[12,2,128,128]{3,2,1,0:T(8,128)} %get-tuple-element.15.fk_hbm, f32[4,2,128,128]{3,2,1,0:T(8,128)} %get-tuple-element.16.fm_hbm, ...), custom_call_target="tpu_custom_call" | custom-call | flops 56000000 | bytes 7000000 | tf_op jit(solution)/shard_map/sweeps/pallas_call | solution.py:467
  46.5 15.4 %all_to_all.15.recv_ref = f32[16,56,128]{2,1,0:T(8,128)S(1)} all-to-all(f32[16,56,128]{2,1,0:T(8,128)S(1)} %get-tuple-element.24), channel_id=1, replica_groups=mesh['gx'=8,'gy'=16] {'gy'}, dimensions={0} | all-to-all | bytes 917504 | tf_op jit(solution)/shard_map/all_to_all | solution.py:491
  62.0 0.6 sums.1
  62.6 6.4 %all-to-all-start.2 = ((f32[8,8,128]{2,1,0:T(8,128)}), f32[8,8,128]{2,1,0:T(8,128)S(1)}, u32[]{:S(2)}, u32[]{:S(2)}) async-start(f32[8,8,128]{2,1,0:T(8,128)} %sums.1), calls=%async_computation.2 | async-start | bytes 65536 | tf_op jit(solution)/shard_map/all_to_all | solution.py:516
  69.0 1.6 %join.1 = f32[3,256,512]{2,1,0:T(8,128)} custom-call(f32[12,2,128,128]{3,2,1,0:T(8,128)S(1)} %get-tuple-element.23.fine_ref), custom_call_target="tpu_custom_call" | custom-call | flops 14000000 | bytes 3000000 | tf_op jit(solution)/shard_map/join/pallas_call | solution.py:493
  70.6 0.8 %coarse.1 = f32[3,8,4096]{2,1,0:T(8,128)} custom-call(f32[16,56,128]{2,1,0:T(8,128)S(1)} %all_to_all.15.recv_ref), custom_call_target="tpu_custom_call" | custom-call | flops 7000000 | bytes 800000 | tf_op jit(solution)/shard_map/coarse/pallas_call | solution.py:517
  71.4 2.3 %all-to-all-done.2 = f32[8,8,128]{2,1,0:T(8,128)S(1)} async-done(((f32[8,8,128]{2,1,0:T(8,128)}), f32[8,8,128]{2,1,0:T(8,128)S(1)}, u32[]{:S(2)}, u32[]{:S(2)}) %all-to-all-start.2) | async-done | bytes 32800 | tf_op jit(solution)/shard_map/all_to_all | solution.py:516
  73.7 0.1 slice_reduce_fusion
  73.8 0.5 multiply_sqrt_fusion
Async XLA Ops:
  2.9 23.9 %all-to-all-start = ((f32[16,120,128]{2,1,0:T(8,128)}), f32[16,120,128]{2,1,0:T(8,128)S(1)}, u32[]{:S(2)}, u32[]{:S(2)}) async-start(f32[16,120,128]{2,1,0:T(8,128)} %pack.1), calls=%async_computation | async-start | bytes 1966080 | tf_op jit(solution)/shard_map/all_to_all | solution.py:423
  17.1 8.2 %collective-permute-start = (f32[128,128]{1,0:T(8,128)S(1)}, f32[128,128]{1,0:T(8,128)S(1)}, u32[]{:S(2)}, u32[]{:S(2)}) collective-permute-start(f32[128,128]{1,0:T(8,128)S(1)} %get-tuple-element.17), channel_id=1, source_target_pairs={{0,1},{1,2},{2,3},{3,4},{4,5},{5,6},{6,7},{7,8},{8,9},{9,10},{10,1... | collective-permute-start | bytes 196616 | tf_op jit(solution)/shard_map/ppermute | solution.py:450
  20.4 6.4 %collective-permute-start.1 = (f32[128,128]{1,0:T(8,128)S(1)}, f32[128,128]{1,0:T(8,128)S(1)}, u32[]{:S(2)}, u32[]{:S(2)}) collective-permute-start(f32[128,128]{1,0:T(8,128)S(1)} %get-tuple-element.18), channel_id=1, source_target_pairs={{1,0},{2,1},{3,2},{4,3},{5,4},{6,5},{7,6},{8,7},{9,8},{10,9},{11,1... | collective-permute-start | bytes 196616 | tf_op jit(solution)/shard_map/ppermute | solution.py:451
  27.0 7.6 %collective-permute-start.2 = (f32[3,64,128]{2,1,0:T(8,128)S(1)}, f32[3,64,128]{2,1,0:T(8,128)S(1)}, u32[]{:S(2)}, u32[]{:S(2)}) collective-permute-start(f32[3,64,128]{2,1,0:T(8,128)S(1)} %get-tuple-element.21), channel_id=1, source_target_pairs={{0,16},{16,32},{32,48},{48,64},{64,80},{80,96},{96,112},{1,17},{17... | collective-permute-start | bytes 294920 | tf_op jit(solution)/shard_map/ppermute | solution.py:464
  32.6 5.9 %collective-permute-start.3 = (f32[3,64,128]{2,1,0:T(8,128)S(1)}, f32[3,64,128]{2,1,0:T(8,128)S(1)}, u32[]{:S(2)}, u32[]{:S(2)}) collective-permute-start(f32[3,64,128]{2,1,0:T(8,128)S(1)} %get-tuple-element.22), channel_id=1, source_target_pairs={{16,0},{32,16},{48,32},{64,48},{80,64},{96,80},{112,96},{17,1},{33... | collective-permute-start | bytes 294920 | tf_op jit(solution)/shard_map/ppermute | solution.py:465
  62.6 11.1 %all-to-all-start.2 = ((f32[8,8,128]{2,1,0:T(8,128)}), f32[8,8,128]{2,1,0:T(8,128)S(1)}, u32[]{:S(2)}, u32[]{:S(2)}) async-start(f32[8,8,128]{2,1,0:T(8,128)} %sums.1), calls=%async_computation.2 | async-start | bytes 65536 | tf_op jit(solution)/shard_map/all_to_all | solution.py:516

commit v3 on v2

--- a/solution.py
+++ b/solution.py
@@ -10,6 +10,7 @@
 BOTH = (GX, GY)
 PR = 128
 TOP = 16
+SPLIT = 64
 ROWS = PR + 40
 F32 = jnp.float32
 BF16 = jnp.bfloat16
@@ -65,19 +66,26 @@
     return tile
 
 
-def pack_kernel(start_hbm, known_hbm, mu_hbm, chunk_ref, start_ref, known_ref, mu_ref, sems):
-    copies = [
-        pltpu.make_async_copy(src, dst, sems.at[n])
-        for n, (src, dst) in enumerate(((start_hbm, start_ref), (known_hbm, known_ref), (mu_hbm, mu_ref)))
-    ]
-    for copy in copies:
+def pack_kernel(start_hbm, known_hbm, mu_hbm, chunk_hbm, start_ref, known_ref, mu_ref, chunk_ref, sems, out_sems):
+    width = start_ref.shape[-1] // 4
+    reads, writes = [], []
+    for n in range(4):
+        cols = pl.ds(n * width, width)
+        for i, (src, dst) in enumerate(((start_hbm, start_ref), (known_hbm, known_ref))):
+            reads.append(pltpu.make_async_copy(src.at[:, :, cols], dst.at[:, :, cols], sems.at[3 * n + i]))
+        reads.append(pltpu.make_async_copy(mu_hbm.at[:, cols], mu_ref.at[:, cols], sems.at[3 * n + 2]))
+    for copy in reads:
         copy.start()
-    for copy in copies:
+    for copy in reads[:3]:
         copy.wait()
     tile = planes_of(start_ref, known_ref, mu_ref)
     lane = lanes_of(8)
     zero = jnp.zeros((8, 128), F32)
     for j in range(16):
+        n = j // 4
+        if j % 4 == 3 and n < 3:
+            for copy in reads[3 * n + 3 : 3 * n + 6]:
+                copy.wait()
         side = zero
         for p in range(7):
             left = tile(p, 2 * j - 1) if j else zero
@@ -87,6 +95,12 @@
             for m in range(2):
                 chunk_ref[j, pl.ds((2 * p + m) * 8, 8), :] = tile(p, 2 * j + m)
         chunk_ref[j, pl.ds(112, 8), :] = side
+        if j % 4 == 3:
+            group = pl.ds(4 * n, 4)
+            writes.append(pltpu.make_async_copy(chunk_ref.at[group], chunk_hbm.at[group], out_sems.at[n]))
+            writes[-1].start()
+    for copy in writes:
+        copy.wait()
 
 
 def beside(x, p):
@@ -205,10 +219,15 @@
     ca, cb, xa, xb, kc, mc, rc, fa, fb, kf, mf, rf, sems,
 ):
     own = pl.ds(TOP, PR)
-    copies = [
-        pltpu.make_async_copy(src, dst.at[:, pl.ds(0, 2), own, :], sems.at[n])
-        for n, (src, dst) in enumerate(((fm_hbm, mf), (fs_hbm, fa), (fk_hbm, kf)))
-    ]
+    copies = []
+    for src, dst, first, last in (
+        (fm_hbm, mf, 0, PR), (fs_hbm, fa, 0, SPLIT + 8), (fk_hbm, kf, 0, SPLIT),
+        (fs_hbm, fa, SPLIT + 8, PR), (fk_hbm, kf, SPLIT, PR),
+    ):
+        rows, place = pl.ds(first, last - first), pl.ds(TOP + first, last - first)
+        copies.append(
+            pltpu.make_async_copy(src.at[:, :, rows, :], dst.at[:, pl.ds(0, 2), place, :], sems.at[len(copies)])
+        )
     for copy in copies:
         copy.start()
     zero8 = jnp.zeros((8, 128), F32)
@@ -285,8 +304,8 @@
             mix(xa, k, r, [ca[k, m, r, :] for m in range(3)])
         return carry
 
-    lax.fori_loop(0, PR // 8 + 2, ready, 0, unroll=6)
-    for copy in copies[1:]:
+    lax.fori_loop(0, PR // 8 + 2, ready, 0, unroll=9)
+    for copy in copies[1:3]:
         copy.wait()
 
     def step(r, c_old, x_old, f_old, store_c, store_f, tiles, sums):
@@ -319,7 +338,7 @@
             store_c(k, new)
         return (totals[0] + totals[1]) + (totals[2] + totals[3])
 
-    def sweep(c_old, x_old, f_old, c_new, x_new, f_new):
+    def sweep(c_old, x_old, f_old, c_new, x_new, f_new, pending):
         def stores(r):
             rows = pl.ds(r, 8)
 
@@ -337,7 +356,11 @@
             r = pl.multiple_of(TOP + 8 * i, 8)
             return total + step(r, c_old, x_old, f_old, *stores(r), 3, True)
 
-        total = lax.fori_loop(0, PR // 8, body, zero8, unroll=4)
+        half = SPLIT // 8
+        total = lax.fori_loop(0, half, body, zero8, unroll=half)
+        for copy in pending:
+            copy.wait()
+        total = lax.fori_loop(half, PR // 8, body, total, unroll=half)
 
         def edge(i, carry):
             r = pl.multiple_of(TOP - 8 + i * (PR + 8), 8)
@@ -347,7 +370,7 @@
         lax.fori_loop(0, 2, edge, 0, unroll=True)
         return total
 
-    totals = [sweep(ca, xa, fa, cb, xb, fb), sweep(cb, xb, fb, ca, xa, fa)]
+    totals = [sweep(ca, xa, fa, cb, xb, fb, copies[3:]), sweep(cb, xb, fb, ca, xa, fa, [])]
 
     def last(i, total):
         r = pl.multiple_of(TOP + 8 * i, 8)
@@ -361,7 +384,7 @@
 
         return total + step(r, ca, xa, fa, store_c, store_f, 2, True)
 
-    totals.append(lax.fori_loop(0, PR // 8, last, zero8, unroll=4))
+    totals.append(lax.fori_loop(0, PR // 8, last, zero8, unroll=8))
     sums = 0.0625 * jnp.concatenate([jnp.sum(v, axis=0, keepdims=True) for v in totals] + [jnp.zeros((5, 128), F32)], axis=0)
     for j in range(16):
         chunk_ref[j, pl.ds(48, 8), :] = sums
@@ -407,14 +430,16 @@
     cell_total = 3.0 * (fine_mu.size + coarse_mu.size) * (count_x * count_y)
     chunk = pl.pallas_call(
         pack_kernel,
-        out_shape=pltpu.VMEM((16, MAIN, 128), F32),
+        out_shape=pltpu.HBM((16, MAIN, 128), F32),
         in_specs=[HBM] * 3,
-        out_specs=VMEM,
+        out_specs=HBM,
         scratch_shapes=[
             pltpu.VMEM(coarse_start.shape, F32),
             pltpu.VMEM(coarse_known.shape, F32),
             pltpu.VMEM(coarse_mu.shape, F32),
-            pltpu.SemaphoreType.DMA((3,)),
+            pltpu.VMEM((16, MAIN, 128), F32),
+            pltpu.SemaphoreType.DMA((12,)),
+            pltpu.SemaphoreType.DMA((4,)),
         ],
         compiler_params=params(GRANT_KIB),
         cost_estimate=cost(2, 2e6),
@@ -482,7 +507,7 @@
             pltpu.VMEM((12, 3, ROWS, 128), F32),
             pltpu.VMEM((4, 3, ROWS, 128), F32),
             pltpu.VMEM((4, 3, ROWS, 128), F32),
-            pltpu.SemaphoreType.DMA((3,)),
+            pltpu.SemaphoreType.DMA((5,)),
         ],
         compiler_params=params(GRANT_KIB),
         cost_estimate=cost(8, 7e6),

time: 74.7 us -> 72.8 us (0.975)
  Pallas kernels: 18.9 us -> 17 us
    pallas_call x1, Pallas kernels: 7.92 us -> 6 us  [on_device(): pl.pallas_call(sweep_kernel, out_shape=(pltpu.VMEM((16, 56, 128), F32), p...]
where the time goes in v3:
time: 72.8 us; the launch traced here: 72.3 us
  starting transfers between devices  27.1 us (37%)
  Pallas kernels  17 us (23%)
  blocking collectives  15.4 us (21%)
  waiting for transfers between devices  11.4 us (16%)
    all_to_all x1, blocking collectives, on_device(): out = lax.all_to_all(chunk, GY, 0, 0, tiled=True)  15.4 us
    all_to_all x1, starting transfers between devices, on_device(): recv = lax.all_to_all(chunk, GY, 0, 0, tiled=True)  8.6 us
    all_to_all x1, starting transfers between devices, on_device(): sums = lax.all_to_all(sums, GX, 0, 0, tiled=True)  6.32 us
    pallas_call x1, Pallas kernels, on_device(): pl.pallas_call(sweep_kernel, out_shape=(pltpu.VMEM((16, 56, 128), F32), p...  6 us
    ppermute x1, starting transfers between devices, on_device(): above = lax.ppermute(down, GX, ahead(count_x))  5.67 us
    pallas_call x1, Pallas kernels, on_device(): pl.pallas_call(fine_kernel, out_shape=(*(pltpu.HBM((n, 2, PR, 128), F32)...  5.57 us
    ppermute x1, waiting for transfers between devices, on_device(): below = lax.ppermute(up, GX, back(count_x))  4 us
    ppermute x1, waiting for transfers between devices, on_device(): left = lax.ppermute(high, GY, ahead(count_y))  3.64 us
  transfers between devices with their start and end apart: 6, of which 4 were waited for; matrix products, arithmetic and copies ran while one was open for 0% of the time, Pallas kernels for 11%

profile of v3, /device:TPU:1, one launch (start us, length us, event | category | flops | bytes accessed | tf_op | source)
XLA Modules:
  0.0 72.3 jit_solution(18346761376515536621)
XLA Ops:
  0.6 2.3 %pack.1 = f32[16,120,128]{2,1,0:T(8,128)} custom-call(f32[3,8,4096]{2,1,0:T(8,128)} %start_hbm.3, f32[3,8,4096]{2,1,0:T(8,128)} %known_hbm.3, f32[8,4096]{1,0:T(8,128)} %mu_hbm.3), custom_call_target="tpu_custom_call" | custom-call | flops 14000000 | bytes 2000000 | tf_op jit(solution)/shard_map/pack/pallas_call | solution.py:431
  2.9 8.6 %all-to-all-start = ((f32[16,120,128]{2,1,0:T(8,128)}), f32[16,120,128]{2,1,0:T(8,128)S(1)}, u32[]{:S(2)}, u32[]{:S(2)}) async-start(f32[16,120,128]{2,1,0:T(8,128)} %pack.1), calls=%async_computation | async-start | bytes 1966080 | tf_op jit(solution)/shard_map/all_to_all | solution.py:448
  11.5 5.6 %fine.1 = (f32[12,2,128,128]{3,2,1,0:T(8,128)}, f32[12,2,128,128]{3,2,1,0:T(8,128)}, f32[4,2,128,128]{3,2,1,0:T(8,128)}, f32[128,128]{1,0:T(8,128)S(1)}, f32[128...) custom-call(f32[3,256,512]{2,1,0:T(8,128)} %start_hbm.2, f32[3,256,512]{2,1,0:T(8,128)} %known_hbm.2, ...), custom_call_target="tpu_custom_call" | custom-call | flops 28000000 | bytes 7000000 | tf_op jit(solution)/shard_map/fine/pallas_call | solution.py:450
  17.1 3.3 %collective-permute-start = (f32[128,128]{1,0:T(8,128)S(1)}, f32[128,128]{1,0:T(8,128)S(1)}, u32[]{:S(2)}, u32[]{:S(2)}) collective-permute-start(f32[128,128]{1,0:T(8,128)S(1)} %get-tuple-element.17), channel_id=1, source_target_pairs={{0,1},{1,2},{2,3},{3,4},{4,5},{5,6},{6,7},{7,8},{8,9},{9,10},{10,1... | collective-permute-start | bytes 196616 | tf_op jit(solution)/shard_map/ppermute | solution.py:475
  20.4 1.3 %collective-permute-start.1 = (f32[128,128]{1,0:T(8,128)S(1)}, f32[128,128]{1,0:T(8,128)S(1)}, u32[]{:S(2)}, u32[]{:S(2)}) collective-permute-start(f32[128,128]{1,0:T(8,128)S(1)} %get-tuple-element.18), channel_id=1, source_target_pairs={{1,0},{2,1},{3,2},{4,3},{5,4},{6,5},{7,6},{8,7},{9,8},{10,9},{11,1... | collective-permute-start | bytes 196616 | tf_op jit(solution)/shard_map/ppermute | solution.py:476
  21.7 3.6 %collective-permute-done.left_ref = f32[128,128]{1,0:T(8,128)S(1)} collective-permute-done((f32[128,128]{1,0:T(8,128)S(1)}, f32[128,128]{1,0:T(8,128)S(1)}, u32[]{:S(2)}, u32[]{:S(2)}) %collective-permute-start) | collective-permute-done | bytes 65568 | tf_op jit(solution)/shard_map/ppermute | solution.py:475
  25.4 1.5 %collective-permute-done.1.right_ref = f32[128,128]{1,0:T(8,128)S(1)} collective-permute-done((f32[128,128]{1,0:T(8,128)S(1)}, f32[128,128]{1,0:T(8,128)S(1)}, u32[]{:S(2)}, u32[]{:S(2)}) %collective-permute-start.1) | collective-permute-done | bytes 65568 | tf_op jit(solution)/shard_map/ppermute | solution.py:476
  26.8 0.0 all-to-all-done.first_ref.last_ref.recv_ref
  26.8 0.1 rows.1
  27.0 5.7 %collective-permute-start.2 = (f32[3,64,128]{2,1,0:T(8,128)S(1)}, f32[3,64,128]{2,1,0:T(8,128)S(1)}, u32[]{:S(2)}, u32[]{:S(2)}) collective-permute-start(f32[3,64,128]{2,1,0:T(8,128)S(1)} %get-tuple-element.21), channel_id=1, source_target_pairs={{0,16},{16,32},{32,48},{48,64},{64,80},{80,96},{96,112},{1,17},{17... | collective-permute-start | bytes 294920 | tf_op jit(solution)/shard_map/ppermute | solution.py:489
  32.6 1.9 %collective-permute-start.3 = (f32[3,64,128]{2,1,0:T(8,128)S(1)}, f32[3,64,128]{2,1,0:T(8,128)S(1)}, u32[]{:S(2)}, u32[]{:S(2)}) collective-permute-start(f32[3,64,128]{2,1,0:T(8,128)S(1)} %get-tuple-element.22), channel_id=1, source_target_pairs={{16,0},{32,16},{48,32},{64,48},{80,64},{96,80},{112,96},{17,1},{33... | collective-permute-start | bytes 294920 | tf_op jit(solution)/shard_map/ppermute | solution.py:490
  34.6 0.0 collective-permute-done.2.above_ref
  34.6 4.0 %collective-permute-done.3.below_ref = f32[3,64,128]{2,1,0:T(8,128)S(1)} collective-permute-done((f32[3,64,128]{2,1,0:T(8,128)S(1)}, f32[3,64,128]{2,1,0:T(8,128)S(1)}, u32[]{:S(2)}, u32[]{:S(2)}) %collective-permute-start.3) | collective-permute-done | bytes 98336 | tf_op jit(solution)/shard_map/ppermute | solution.py:490
  38.6 6.0 %sweeps.1 = (f32[16,56,128]{2,1,0:T(8,128)S(1)}, f32[12,2,128,128]{3,2,1,0:T(8,128)S(1)}) custom-call(f32[12,2,128,128]{3,2,1,0:T(8,128)} %get-tuple-element.14.fs_hbm, f32[12,2,128,128]{3,2,1,0:T(8,128)} %get-tuple-element.15.fk_hbm, f32[4,2,128,128]{3,2,1,0:T(8,128)} %get-tuple-element.16.fm_hbm, ...), custom_call_target="tpu_custom_call" | custom-call | flops 56000000 | bytes 7000000 | tf_op jit(solution)/shard_map/sweeps/pallas_call | solution.py:492
  44.6 15.4 %all_to_all.15.recv_ref = f32[16,56,128]{2,1,0:T(8,128)S(1)} all-to-all(f32[16,56,128]{2,1,0:T(8,128)S(1)} %get-tuple-element.24), channel_id=1, replica_groups=mesh['gx'=8,'gy'=16] {'gy'}, dimensions={0} | all-to-all | bytes 917504 | tf_op jit(solution)/shard_map/all_to_all | solution.py:516
  60.0 0.6 sums.1
  60.7 6.3 %all-to-all-start.2 = ((f32[8,8,128]{2,1,0:T(8,128)}), f32[8,8,128]{2,1,0:T(8,128)S(1)}, u32[]{:S(2)}, u32[]{:S(2)}) async-start(f32[8,8,128]{2,1,0:T(8,128)} %sums.1), calls=%async_computation.2 | async-start | bytes 65536 | tf_op jit(solution)/shard_map/all_to_all | solution.py:541
  67.0 1.6 %join.1 = f32[3,256,512]{2,1,0:T(8,128)} custom-call(f32[12,2,128,128]{3,2,1,0:T(8,128)S(1)} %get-tuple-element.23.fine_ref), custom_call_target="tpu_custom_call" | custom-call | flops 14000000 | bytes 3000000 | tf_op jit(solution)/shard_map/join/pallas_call | solution.py:518
  68.6 0.8 %coarse.1 = f32[3,8,4096]{2,1,0:T(8,128)} custom-call(f32[16,56,128]{2,1,0:T(8,128)S(1)} %all_to_all.15.recv_ref), custom_call_target="tpu_custom_call" | custom-call | flops 7000000 | bytes 800000 | tf_op jit(solution)/shard_map/coarse/pallas_call | solution.py:542
  69.4 2.3 %all-to-all-done.2 = f32[8,8,128]{2,1,0:T(8,128)S(1)} async-done(((f32[8,8,128]{2,1,0:T(8,128)}), f32[8,8,128]{2,1,0:T(8,128)S(1)}, u32[]{:S(2)}, u32[]{:S(2)}) %all-to-all-start.2) | async-done | bytes 32800 | tf_op jit(solution)/shard_map/all_to_all | solution.py:541
  71.7 0.1 slice_reduce_fusion
  71.8 0.5 multiply_sqrt_fusion
Async XLA Ops:
  2.9 23.9 %all-to-all-start = ((f32[16,120,128]{2,1,0:T(8,128)}), f32[16,120,128]{2,1,0:T(8,128)S(1)}, u32[]{:S(2)}, u32[]{:S(2)}) async-start(f32[16,120,128]{2,1,0:T(8,128)} %pack.1), calls=%async_computation | async-start | bytes 1966080 | tf_op jit(solution)/shard_map/all_to_all | solution.py:448
  17.1 8.2 %collective-permute-start = (f32[128,128]{1,0:T(8,128)S(1)}, f32[128,128]{1,0:T(8,128)S(1)}, u32[]{:S(2)}, u32[]{:S(2)}) collective-permute-start(f32[128,128]{1,0:T(8,128)S(1)} %get-tuple-element.17), channel_id=1, source_target_pairs={{0,1},{1,2},{2,3},{3,4},{4,5},{5,6},{6,7},{7,8},{8,9},{9,10},{10,1... | collective-permute-start | bytes 196616 | tf_op jit(solution)/shard_map/ppermute | solution.py:475
  20.4 6.4 %collective-permute-start.1 = (f32[128,128]{1,0:T(8,128)S(1)}, f32[128,128]{1,0:T(8,128)S(1)}, u32[]{:S(2)}, u32[]{:S(2)}) collective-permute-start(f32[128,128]{1,0:T(8,128)S(1)} %get-tuple-element.18), channel_id=1, source_target_pairs={{1,0},{2,1},{3,2},{4,3},{5,4},{6,5},{7,6},{8,7},{9,8},{10,9},{11,1... | collective-permute-start | bytes 196616 | tf_op jit(solution)/shard_map/ppermute | solution.py:476
  27.0 7.6 %collective-permute-start.2 = (f32[3,64,128]{2,1,0:T(8,128)S(1)}, f32[3,64,128]{2,1,0:T(8,128)S(1)}, u32[]{:S(2)}, u32[]{:S(2)}) collective-permute-start(f32[3,64,128]{2,1,0:T(8,128)S(1)} %get-tuple-element.21), channel_id=1, source_target_pairs={{0,16},{16,32},{32,48},{48,64},{64,80},{80,96},{96,112},{1,17},{17... | collective-permute-start | bytes 294920 | tf_op jit(solution)/shard_map/ppermute | solution.py:489
  32.6 5.9 %collective-permute-start.3 = (f32[3,64,128]{2,1,0:T(8,128)S(1)}, f32[3,64,128]{2,1,0:T(8,128)S(1)}, u32[]{:S(2)}, u32[]{:S(2)}) collective-permute-start(f32[3,64,128]{2,1,0:T(8,128)S(1)} %get-tuple-element.22), channel_id=1, source_target_pairs={{16,0},{32,16},{48,32},{64,48},{80,64},{96,80},{112,96},{17,1},{33... | collective-permute-start | bytes 294920 | tf_op jit(solution)/shard_map/ppermute | solution.py:490
  60.7 11.0 %all-to-all-start.2 = ((f32[8,8,128]{2,1,0:T(8,128)}), f32[8,8,128]{2,1,0:T(8,128)S(1)}, u32[]{:S(2)}, u32[]{:S(2)}) async-start(f32[8,8,128]{2,1,0:T(8,128)} %sums.1), calls=%async_computation.2 | async-start | bytes 65536 | tf_op jit(solution)/shard_map/all_to_all | solution.py:541

commit v4 on v3

--- a/solution.py
+++ b/solution.py
@@ -47,7 +47,8 @@
 
 
 MAIN = 120
-EDGE = 64
+TILE_ROWS = 57
+PAIR, SIDE, EDGE = 2 * TILE_ROWS, 2 * TILE_ROWS + 2, 120
 
 
 def edge_rows(p):
@@ -196,21 +197,17 @@
 
 
 def rows_kernel(left_ref, right_ref, top_ref, bottom_ref, first_ref, last_ref, up_ref, down_ref):
-    for part, patch, out, two, one in ((top_ref, first_ref, up_ref, 0, 0), (bottom_ref, last_ref, down_ref, 126, 127)):
-        out[0:2, 0:40, :] = part[...]
-        pair = left_ref[two : two + 2] + right_ref[two : two + 2]
-        single = left_ref[one : one + 1] + right_ref[one : one + 1]
-        for t in range(12):
-            out[2, pl.ds(2 * t, 2), :] = start_side(pair, t)
-            out[2, pl.ds(24 + t, 1), :] = other_side(single, 48 + 2 * t)
-        for t in range(4):
-            out[2, pl.ds(36 + t, 1), :] = other_side(single, 72 + 2 * t)
-        for p in range(7):
-            row, count = edge_rows(p)
-            at = 0 if one == 0 else 8 - count
-            for m in range(2):
-                out[m, pl.ds(row, count), :] = patch[0, pl.ds((2 * p + m) * 8 + at, count), :]
-            out[2, pl.ds(row, count), :] = beside(patch[0, pl.ds(112 + at, count), :], p)
+    for part, patch, out, low in ((top_ref, first_ref, up_ref, True), (bottom_ref, last_ref, down_ref, False)):
+        two = 0 if low else PR - 2
+        for m in range(2):
+            out[pl.ds(m * TILE_ROWS, 40), :] = part[m]
+            for p in range(7):
+                row, count = edge_rows(p)
+                at = (2 * p + m) * 8 + (0 if low else 8 - count)
+                out[pl.ds(m * TILE_ROWS + row, count), :] = patch[0, pl.ds(at, count), :]
+        out[pl.ds(PAIR, 2), :] = left_ref[two : two + 2] + right_ref[two : two + 2]
+        out[pl.ds(SIDE, 3), :] = patch[0, pl.ds(112 if low else 117, 3), :]
+        out[pl.ds(SIDE + 3, 1), :] = jnp.zeros((1, 128), F32)
 
 
 def sweep_kernel(
@@ -252,24 +249,34 @@
                 ref[m, rows, :] = recv_ref[j, pl.ds((2 * p + m) * 8, 8), :]
             ref[2, rows, :] = beside(recv_ref[j, pl.ds(112, 8), :], p)
         row, count = edge_rows(p)
-        for m in range(3):
-            ref[m, pl.ds(TOP - count, count), :] = above_ref[m, pl.ds(row, count), :]
-            ref[m, pl.ds(TOP + PR, count), :] = below_ref[m, pl.ds(row, count), :]
+        for m in range(2):
+            ref[m, pl.ds(TOP - count, count), :] = above_ref[pl.ds(m * TILE_ROWS + row, count), :]
+            ref[m, pl.ds(TOP + PR, count), :] = below_ref[pl.ds(m * TILE_ROWS + row, count), :]
+        ref[2, pl.ds(TOP - count, count), :] = beside(above_ref[pl.ds(SIDE + 3 - count, count), :], p)
+        ref[2, pl.ds(TOP + PR, count), :] = beside(below_ref[pl.ds(SIDE, count), :], p)
     both = left_ref[...] + right_ref[...]
     for t in range(12):
         fa[t, 2, own, :] = start_side(both, t)
         kf[t, 2, own, :] = other_side(both, 48 + 2 * t)
     for t in range(4):
         mf[t, 2, own, :] = other_side(both, 72 + 2 * t)
-    for m in range(3):
+    for m in range(2):
+        at = m * TILE_ROWS
         for t in range(12):
-            fa[t, m, pl.ds(TOP - 2, 2), :] = above_ref[m, pl.ds(2 * t, 2), :]
-            fa[t, m, pl.ds(TOP + PR, 2), :] = below_ref[m, pl.ds(2 * t, 2), :]
-            kf[t, m, pl.ds(TOP - 1, 1), :] = above_ref[m, pl.ds(24 + t, 1), :]
-            kf[t, m, pl.ds(TOP + PR, 1), :] = below_ref[m, pl.ds(24 + t, 1), :]
+            fa[t, m, pl.ds(TOP - 2, 2), :] = above_ref[pl.ds(at + 2 * t, 2), :]
+            fa[t, m, pl.ds(TOP + PR, 2), :] = below_ref[pl.ds(at + 2 * t, 2), :]
+            kf[t, m, pl.ds(TOP - 1, 1), :] = above_ref[pl.ds(at + 24 + t, 1), :]
+            kf[t, m, pl.ds(TOP + PR, 1), :] = below_ref[pl.ds(at + 24 + t, 1), :]
         for t in range(4):
-            mf[t, m, pl.ds(TOP - 1, 1), :] = above_ref[m, pl.ds(36 + t, 1), :]
-            mf[t, m, pl.ds(TOP + PR, 1), :] = below_ref[m, pl.ds(36 + t, 1), :]
+            mf[t, m, pl.ds(TOP - 1, 1), :] = above_ref[pl.ds(at + 36 + t, 1), :]
+            mf[t, m, pl.ds(TOP + PR, 1), :] = below_ref[pl.ds(at + 36 + t, 1), :]
+    for edge_ref, two, one, near in ((above_ref, TOP - 2, TOP - 1, 1), (below_ref, TOP + PR, TOP + PR, 0)):
+        pair, single = edge_ref[pl.ds(PAIR, 2), :], edge_ref[pl.ds(PAIR + near, 1), :]
+        for t in range(12):
+            fa[t, 2, pl.ds(two, 2), :] = start_side(pair, t)
+            kf[t, 2, pl.ds(one, 1), :] = other_side(single, 48 + 2 * t)
+        for t in range(4):
+            mf[t, 2, pl.ds(one, 1), :] = other_side(single, 72 + 2 * t)
     copies[0].wait()
 
     at_start, at_end = lane8 == 0, lane8 == 127
@@ -304,7 +311,7 @@
             mix(xa, k, r, [ca[k, m, r, :] for m in range(3)])
         return carry
 
-    lax.fori_loop(0, PR // 8 + 2, ready, 0, unroll=9)
+    lax.fori_loop(0, PR // 8 + 2, ready, 0, unroll=18)
     for copy in copies[1:3]:
         copy.wait()
 
@@ -384,7 +391,7 @@
 
         return total + step(r, ca, xa, fa, store_c, store_f, 2, True)
 
-    totals.append(lax.fori_loop(0, PR // 8, last, zero8, unroll=8))
+    totals.append(lax.fori_loop(0, PR // 8, last, zero8, unroll=16))
     sums = 0.0625 * jnp.concatenate([jnp.sum(v, axis=0, keepdims=True) for v in totals] + [jnp.zeros((5, 128), F32)], axis=0)
     for j in range(16):
         chunk_ref[j, pl.ds(48, 8), :] = sums
@@ -477,11 +484,11 @@
     up, down = pl.pallas_call(
         rows_kernel,
         grid=(1,),
-        out_shape=(shaped(3, EDGE, 128),) * 2,
+        out_shape=(shaped(EDGE, 128),) * 2,
         in_specs=[pl.BlockSpec((PR, 128), lambda i: (0, 0))] * 2
         + [pl.BlockSpec((2, 40, 128), lambda i: (0, 0, 0))] * 2
         + [pl.BlockSpec((1, MAIN, 128), lambda i: (0, 0, 0)), pl.BlockSpec((1, MAIN, 128), lambda i: (15, 0, 0))],
-        out_specs=(pl.BlockSpec((3, EDGE, 128), lambda i: (0, 0, 0)),) * 2,
+        out_specs=(pl.BlockSpec((EDGE, 128), lambda i: (0, 0)),) * 2,
         compiler_params=params(GRANT_KIB),
         cost_estimate=cost(1, 0.3e6),
         name="rows",

time: 72.8 us -> 72 us (0.989)
  no operation moved by 1% of the time
where the time goes in v4:
time: 72 us; the launch traced here: 71.5 us
  starting transfers between devices  26.9 us (37%)
  Pallas kernels  16.5 us (23%)
  blocking collectives  15.8 us (22%)
  waiting for transfers between devices  11 us (15%)
  between operations  0.72 us (1%)
    all_to_all x1, blocking collectives, on_device(): out = lax.all_to_all(chunk, GY, 0, 0, tiled=True)  15.8 us
    all_to_all x1, starting transfers between devices, on_device(): recv = lax.all_to_all(chunk, GY, 0, 0, tiled=True)  8.6 us
    all_to_all x1, starting transfers between devices, on_device(): sums = lax.all_to_all(sums, GX, 0, 0, tiled=True)  6.11 us
    ppermute x1, starting transfers between devices, on_device(): above = lax.ppermute(down, GX, ahead(count_x))  5.67 us
    pallas_call x1, Pallas kernels, on_device(): pl.pallas_call(sweep_kernel, out_shape=(pltpu.VMEM((16, 56, 128), F32), p...  5.59 us
    pallas_call x1, Pallas kernels, on_device(): pl.pallas_call(fine_kernel, out_shape=(*(pltpu.HBM((n, 2, PR, 128), F32)...  5.57 us
    ppermute x1, waiting for transfers between devices, on_device(): left = lax.ppermute(high, GY, ahead(count_y))  3.64 us
    ppermute x1, waiting for transfers between devices, on_device(): below = lax.ppermute(up, GX, back(count_x))  3.6 us
  transfers between devices with their start and end apart: 6, of which 4 were waited for; matrix products, arithmetic and copies ran while one was open for 0% of the time, Pallas kernels for 11%

profile of v4, /device:TPU:1, one launch (start us, length us, event | category | flops | bytes accessed | tf_op | source)
XLA Modules:
  0.0 71.5 jit_solution(7540060529070885513)
XLA Ops:
  0.6 2.3 %pack.1 = f32[16,120,128]{2,1,0:T(8,128)} custom-call(f32[3,8,4096]{2,1,0:T(8,128)} %start_hbm.3, f32[3,8,4096]{2,1,0:T(8,128)} %known_hbm.3, f32[8,4096]{1,0:T(8,128)} %mu_hbm.3), custom_call_target="tpu_custom_call" | custom-call | flops 14000000 | bytes 2000000 | tf_op jit(solution)/shard_map/pack/pallas_call | solution.py:438
  2.9 8.6 %all-to-all-start = ((f32[16,120,128]{2,1,0:T(8,128)}), f32[16,120,128]{2,1,0:T(8,128)S(1)}, u32[]{:S(2)}, u32[]{:S(2)}) async-start(f32[16,120,128]{2,1,0:T(8,128)} %pack.1), calls=%async_computation | async-start | bytes 1966080 | tf_op jit(solution)/shard_map/all_to_all | solution.py:455
  11.5 5.6 %fine.1 = (f32[12,2,128,128]{3,2,1,0:T(8,128)}, f32[12,2,128,128]{3,2,1,0:T(8,128)}, f32[4,2,128,128]{3,2,1,0:T(8,128)}, f32[128,128]{1,0:T(8,128)S(1)}, f32[128...) custom-call(f32[3,256,512]{2,1,0:T(8,128)} %start_hbm.2, f32[3,256,512]{2,1,0:T(8,128)} %known_hbm.2, ...), custom_call_target="tpu_custom_call" | custom-call | flops 28000000 | bytes 7000000 | tf_op jit(solution)/shard_map/fine/pallas_call | solution.py:457
  17.1 3.3 %collective-permute-start = (f32[128,128]{1,0:T(8,128)S(1)}, f32[128,128]{1,0:T(8,128)S(1)}, u32[]{:S(2)}, u32[]{:S(2)}) collective-permute-start(f32[128,128]{1,0:T(8,128)S(1)} %get-tuple-element.17), channel_id=1, source_target_pairs={{0,1},{1,2},{2,3},{3,4},{4,5},{5,6},{6,7},{7,8},{8,9},{9,10},{10,1... | collective-permute-start | bytes 196616 | tf_op jit(solution)/shard_map/ppermute | solution.py:482
  20.4 1.3 %collective-permute-start.1 = (f32[128,128]{1,0:T(8,128)S(1)}, f32[128,128]{1,0:T(8,128)S(1)}, u32[]{:S(2)}, u32[]{:S(2)}) collective-permute-start(f32[128,128]{1,0:T(8,128)S(1)} %get-tuple-element.18), channel_id=1, source_target_pairs={{1,0},{2,1},{3,2},{4,3},{5,4},{6,5},{7,6},{8,7},{9,8},{10,9},{11,1... | collective-permute-start | bytes 196616 | tf_op jit(solution)/shard_map/ppermute | solution.py:483
  21.7 3.6 %collective-permute-done.left_ref = f32[128,128]{1,0:T(8,128)S(1)} collective-permute-done((f32[128,128]{1,0:T(8,128)S(1)}, f32[128,128]{1,0:T(8,128)S(1)}, u32[]{:S(2)}, u32[]{:S(2)}) %collective-permute-start) | collective-permute-done | bytes 65568 | tf_op jit(solution)/shard_map/ppermute | solution.py:482
  25.4 1.5 %collective-permute-done.1.right_ref = f32[128,128]{1,0:T(8,128)S(1)} collective-permute-done((f32[128,128]{1,0:T(8,128)S(1)}, f32[128,128]{1,0:T(8,128)S(1)}, u32[]{:S(2)}, u32[]{:S(2)}) %collective-permute-start.1) | collective-permute-done | bytes 65568 | tf_op jit(solution)/shard_map/ppermute | solution.py:483
  26.8 0.0 all-to-all-done.first_ref.last_ref.recv_ref
  26.8 5.7 %collective-permute-start.2 = (f32[120,128]{1,0:T(8,128)S(1)}, f32[120,128]{1,0:T(8,128)S(1)}, u32[]{:S(2)}, u32[]{:S(2)}) collective-permute-start(f32[120,128]{1,0:T(8,128)S(1)} %get-tuple-element.21), channel_id=1, source_target_pairs={{0,16},{16,32},{32,48},{48,64},{64,80},{80,96},{96,112},{1,17},{17... | collective-permute-start | bytes 184328 | tf_op jit(solution)/shard_map/ppermute | solution.py:496
  32.5 1.9 %collective-permute-start.3 = (f32[120,128]{1,0:T(8,128)S(1)}, f32[120,128]{1,0:T(8,128)S(1)}, u32[]{:S(2)}, u32[]{:S(2)}) collective-permute-start(f32[120,128]{1,0:T(8,128)S(1)} %get-tuple-element.22), channel_id=1, source_target_pairs={{16,0},{32,16},{48,32},{64,48},{80,64},{96,80},{112,96},{17,1},{33... | collective-permute-start | bytes 184328 | tf_op jit(solution)/shard_map/ppermute | solution.py:497
  34.5 0.0 collective-permute-done.2.above_ref
  34.5 3.6 %collective-permute-done.3.below_ref = f32[120,128]{1,0:T(8,128)S(1)} collective-permute-done((f32[120,128]{1,0:T(8,128)S(1)}, f32[120,128]{1,0:T(8,128)S(1)}, u32[]{:S(2)}, u32[]{:S(2)}) %collective-permute-start.3) | collective-permute-done | bytes 61472 | tf_op jit(solution)/shard_map/ppermute | solution.py:497
  38.1 5.6 %sweeps.1 = (f32[16,56,128]{2,1,0:T(8,128)S(1)}, f32[12,2,128,128]{3,2,1,0:T(8,128)S(1)}) custom-call(f32[12,2,128,128]{3,2,1,0:T(8,128)} %get-tuple-element.14.fs_hbm, f32[12,2,128,128]{3,2,1,0:T(8,128)} %get-tuple-element.15.fk_hbm, f32[4,2,128,128]{3,2,1,0:T(8,128)} %get-tuple-element.16.fm_hbm, ...), custom_call_target="tpu_custom_call" | custom-call | flops 56000000 | bytes 7000000 | tf_op jit(solution)/shard_map/sweeps/pallas_call | solution.py:499
  43.7 15.8 %all_to_all.15.recv_ref = f32[16,56,128]{2,1,0:T(8,128)S(1)} all-to-all(f32[16,56,128]{2,1,0:T(8,128)S(1)} %get-tuple-element.24), channel_id=1, replica_groups=mesh['gx'=8,'gy'=16] {'gy'}, dimensions={0} | all-to-all | bytes 917504 | tf_op jit(solution)/shard_map/all_to_all | solution.py:523
  59.4 0.6 sums.1
  60.1 6.1 %all-to-all-start.2 = ((f32[8,8,128]{2,1,0:T(8,128)}), f32[8,8,128]{2,1,0:T(8,128)S(1)}, u32[]{:S(2)}, u32[]{:S(2)}) async-start(f32[8,8,128]{2,1,0:T(8,128)} %sums.1), calls=%async_computation.2 | async-start | bytes 65536 | tf_op jit(solution)/shard_map/all_to_all | solution.py:548
  66.2 1.6 %join.1 = f32[3,256,512]{2,1,0:T(8,128)} custom-call(f32[12,2,128,128]{3,2,1,0:T(8,128)S(1)} %get-tuple-element.23.fine_ref), custom_call_target="tpu_custom_call" | custom-call | flops 14000000 | bytes 3000000 | tf_op jit(solution)/shard_map/join/pallas_call | solution.py:525
  67.8 0.8 %coarse.1 = f32[3,8,4096]{2,1,0:T(8,128)} custom-call(f32[16,56,128]{2,1,0:T(8,128)S(1)} %all_to_all.15.recv_ref), custom_call_target="tpu_custom_call" | custom-call | flops 7000000 | bytes 800000 | tf_op jit(solution)/shard_map/coarse/pallas_call | solution.py:549
  68.6 2.3 %all-to-all-done.2 = f32[8,8,128]{2,1,0:T(8,128)S(1)} async-done(((f32[8,8,128]{2,1,0:T(8,128)}), f32[8,8,128]{2,1,0:T(8,128)S(1)}, u32[]{:S(2)}, u32[]{:S(2)}) %all-to-all-start.2) | async-done | bytes 32800 | tf_op jit(solution)/shard_map/all_to_all | solution.py:548
  70.9 0.1 slice_reduce_fusion
  71.0 0.5 multiply_sqrt_fusion
  (1 shorter events, 0.0 us)
Async XLA Ops:
  2.9 23.9 %all-to-all-start = ((f32[16,120,128]{2,1,0:T(8,128)}), f32[16,120,128]{2,1,0:T(8,128)S(1)}, u32[]{:S(2)}, u32[]{:S(2)}) async-start(f32[16,120,128]{2,1,0:T(8,128)} %pack.1), calls=%async_computation | async-start | bytes 1966080 | tf_op jit(solution)/shard_map/all_to_all | solution.py:455
  17.1 8.2 %collective-permute-start = (f32[128,128]{1,0:T(8,128)S(1)}, f32[128,128]{1,0:T(8,128)S(1)}, u32[]{:S(2)}, u32[]{:S(2)}) collective-permute-start(f32[128,128]{1,0:T(8,128)S(1)} %get-tuple-element.17), channel_id=1, source_target_pairs={{0,1},{1,2},{2,3},{3,4},{4,5},{5,6},{6,7},{7,8},{8,9},{9,10},{10,1... | collective-permute-start | bytes 196616 | tf_op jit(solution)/shard_map/ppermute | solution.py:482
  20.4 6.4 %collective-permute-start.1 = (f32[128,128]{1,0:T(8,128)S(1)}, f32[128,128]{1,0:T(8,128)S(1)}, u32[]{:S(2)}, u32[]{:S(2)}) collective-permute-start(f32[128,128]{1,0:T(8,128)S(1)} %get-tuple-element.18), channel_id=1, source_target_pairs={{1,0},{2,1},{3,2},{4,3},{5,4},{6,5},{7,6},{8,7},{9,8},{10,9},{11,1... | collective-permute-start | bytes 196616 | tf_op jit(solution)/shard_map/ppermute | solution.py:483
  26.8 7.6 %collective-permute-start.2 = (f32[120,128]{1,0:T(8,128)S(1)}, f32[120,128]{1,0:T(8,128)S(1)}, u32[]{:S(2)}, u32[]{:S(2)}) collective-permute-start(f32[120,128]{1,0:T(8,128)S(1)} %get-tuple-element.21), channel_id=1, source_target_pairs={{0,16},{16,32},{32,48},{48,64},{64,80},{80,96},{96,112},{1,17},{17... | collective-permute-start | bytes 184328 | tf_op jit(solution)/shard_map/ppermute | solution.py:496
  32.5 5.5 %collective-permute-start.3 = (f32[120,128]{1,0:T(8,128)S(1)}, f32[120,128]{1,0:T(8,128)S(1)}, u32[]{:S(2)}, u32[]{:S(2)}) collective-permute-start(f32[120,128]{1,0:T(8,128)S(1)} %get-tuple-element.22), channel_id=1, source_target_pairs={{16,0},{32,16},{48,32},{64,48},{80,64},{96,80},{112,96},{17,1},{33... | collective-permute-start | bytes 184328 | tf_op jit(solution)/shard_map/ppermute | solution.py:497
  60.1 10.8 %all-to-all-start.2 = ((f32[8,8,128]{2,1,0:T(8,128)}), f32[8,8,128]{2,1,0:T(8,128)S(1)}, u32[]{:S(2)}, u32[]{:S(2)}) async-start(f32[8,8,128]{2,1,0:T(8,128)} %sums.1), calls=%async_computation.2 | async-start | bytes 65536 | tf_op jit(solution)/shard_map/all_to_all | solution.py:548
